TPU v7x, 128 devices: a whole 4x4x4 slice. The times are simulated.
128 devices in a mesh: gx: 8 (over x, core), gy: 16 (over z, y).
Axes of the slice: x: 4, y: 4, z: 4, core: 2. Of those that a mesh axis runs over, the one named last changes fastest.
Arguments:
- samples: bfloat16 [128, 256, 32, 256], P('gx', 'gy'), may hold values from -6 to 6
- leaf_basis: bfloat16 [64, 256], replicated, may hold values from -0.375 to 0.375
- transfer: bfloat16 [5, 64, 256], replicated, may hold values from -0.5 to 0.5
- coupling: bfloat16 [5, 7, 64, 448], replicated, may hold values from -0.15625 to 0.15625
- near_tiles: bfloat16 [9, 256, 256], replicated, may hold values from -0.125 to 0.125
- codes_local: int32 [128, 256, 4, 27], P('gx', 'gy'), may hold values from 0 to 35, as said below
- counts_local: int32 [128, 256, 4], P('gx', 'gy'), may hold values from 1 to 27, as said below
- codes_upper: int32 [168, 27], replicated, may hold values from 0 to 35, as said below
- counts_upper: int32 [168], replicated, may hold values from 1 to 27, as said below
Outputs:
- response: bfloat16 [128, 256, 32, 256], P('gx', 'gy')
Inputs may be any that keep to these rules, and one draw needn't show every extreme that they name: `codes_local`: entries [i, j, l, :] with i and j multiples of 2^l hold the list of the level-l cluster whose first leaf is (i, j); other entries are not read. Its first count entries are distinct codes a * 6 + b of clusters more than one step away from the target in some direction. `counts_local`: length of the list stored at the same position. `codes_upper`: row n is the list of the n-th cluster of level 4 and coarser, levels in order from 4, row-major within a level, each level with half the rows and columns of the one before and the last with 2 rows; first count entries distinct codes of clusters more than one step away from the target in some direction. `counts_upper`: length of the list of the same row.
All inputs are finite; a program needn't handle non-finite values.
Results may differ from a plain program's by a relative error of at most 0.0095.
Values may be sent and summed in bfloat16 or wider, within the bound.
No kernel may reach another device: no remote copies, remote signals or barrier semaphores. Data moves between devices by JAX's collectives and lax.ppermute only.
A program may use at most 384 MiB of HBM per device.

v0:
```python
import jax
import jax.numpy as jnp
from jax import lax
from jax.sharding import Mesh
from jax.sharding import PartitionSpec as P

GX_GY = ("gx_0", "gx_1", "gy_0", "gy_1")
GX = ("gx_0", "gx_1")
GY = ("gy_0", "gy_1")


def extended(block, sides, width):
    for axis, dim in sides:
        count = lax.axis_size(axis)
        forward = [(i, i + 1) for i in range(count - 1)]
        backward = [(target, source) for source, target in forward]
        low = lax.ppermute(
            lax.slice_in_dim(block, block.shape[dim] - width, None, axis=dim), axis, forward
        )
        high = lax.ppermute(lax.slice_in_dim(block, 0, width, axis=dim), axis, backward)
        block = jnp.concatenate([low, block, high], axis=dim)
    return block


def joined_along(blocks, dim):
    blocks = jnp.moveaxis(blocks, 0, dim)
    lengths = blocks.shape
    return blocks.reshape(*lengths[:dim], lengths[dim] * lengths[dim + 1], *lengths[dim + 2 :])


def stacked_from(value, axes, sequence):
    blocks = value[None]
    for k in sequence:
        blocks = lax.all_gather(blocks, axes[k], axis=0, tiled=True)
    current = [lax.axis_size(axes[k]) for k in reversed(sequence)]
    blocks = blocks.reshape(*current, *value.shape)
    turned = sorted(range(len(sequence)), key=lambda place: sequence[len(sequence) - 1 - place])
    return blocks.transpose(*turned, *range(len(sequence), blocks.ndim)).reshape(-1, *value.shape)


def gathered_by_axis(value, axes, sequence, dim):
    return joined_along(stacked_from(value, axes, sequence), dim)


def is_near(row_step, col_step):
    return abs(row_step) <= 1 and abs(col_step) <= 1


def project(leaf_samples, leaf_basis):
    coeffs = jnp.einsum(
        "ijvs,rs->ijvr", leaf_samples, leaf_basis, preferred_element_type=jnp.float32
    )
    return coeffs.astype(jnp.bfloat16)


def lift_level(children, matrices):
    grid_rows, grid_cols, vectors, rank_size = children.shape
    grouped = children.reshape(grid_rows // 2, 2, grid_cols // 2, 2, vectors, rank_size)
    grouped = grouped.transpose(0, 2, 4, 1, 3, 5).reshape(
        grid_rows // 2, grid_cols // 2, vectors, 4 * rank_size
    )
    parent = jnp.einsum("pqvc,sc->pqvs", grouped, matrices, preferred_element_type=jnp.float32)
    return parent.astype(jnp.bfloat16)


def spread(parent, matrices):
    grid_rows, grid_cols, vectors, rank_size = parent.shape
    carried = jnp.einsum("pqvs,sc->pqvc", parent, matrices, preferred_element_type=jnp.float32)
    carried = carried.reshape(grid_rows, grid_cols, vectors, 2, 2, rank_size).transpose(
        0, 3, 1, 4, 2, 5
    )
    return carried.reshape(2 * grid_rows, 2 * grid_cols, vectors, rank_size)


def member_table(list_codes, counts):
    slot_index = jnp.arange(list_codes.shape[-1], dtype=jnp.int32)
    active = slot_index < counts[..., None]
    matches = (list_codes[..., None] == jnp.arange(36, dtype=jnp.int32)) & active[..., None]
    return jnp.any(matches, axis=-2).astype(jnp.float32)


def couple(padded, member, matrices):
    grid_rows = padded.shape[0] - 4
    grid_cols = padded.shape[1] - 4
    vectors = padded.shape[2]
    rank_size = padded.shape[3]
    member = member.reshape(grid_rows // 2, 2, grid_cols // 2, 2, 36)
    totals = [
        [
            jnp.zeros((grid_rows // 2, grid_cols // 2, vectors, rank_size), jnp.float32)
            for col_bit in range(2)
        ]
        for row_bit in range(2)
    ]
    for code_row in range(6):
        for code_col in range(6):
            parities = [
                (row_bit, col_bit)
                for row_bit in range(2)
                for col_bit in range(2)
                if not is_near(code_row - 2 - row_bit, code_col - 2 - col_bit)
            ]
            if not parities:
                continue
            source = padded[
                code_row : code_row + grid_rows : 2, code_col : code_col + grid_cols : 2
            ]
            blocks = jnp.concatenate(
                [
                    matrices[
                        code_row + 1 - row_bit,
                        :,
                        (code_col + 1 - col_bit) * rank_size : (code_col + 2 - col_bit) * rank_size,
                    ]
                    for row_bit, col_bit in parities
                ],
                axis=0,
            )
            images = jnp.einsum("pqvr,sr->pqvs", source, blocks, preferred_element_type=jnp.float32)
            for number, (row_bit, col_bit) in enumerate(parities):
                weight_mask = member[:, row_bit, :, col_bit, code_row * 6 + code_col]
                totals[row_bit][col_bit] = (
                    totals[row_bit][col_bit]
                    + weight_mask[..., None, None]
                    * images[..., number * rank_size : (number + 1) * rank_size]
                )
    stacked = jnp.stack([jnp.stack(totals[row_bit], axis=0) for row_bit in range(2)], axis=0)
    return stacked.transpose(2, 0, 3, 1, 4, 5).reshape(grid_rows, grid_cols, vectors, rank_size)


def couple_one(padded, member, matrices, row_here, col_here):
    vectors = padded.shape[2]
    rank_size = padded.shape[3]
    window = lax.dynamic_slice(
        padded, (2 * (row_here // 2), 2 * (col_here // 2), 0, 0), (6, 6, vectors, rank_size)
    )
    row_bit = row_here % 2
    col_bit = col_here % 2
    summed = jnp.zeros((vectors, rank_size), jnp.float32)
    for code_row in range(6):
        for code_col in range(6):
            coupling_block = lax.dynamic_slice(
                matrices,
                (code_row + 1 - row_bit, 0, (code_col + 1 - col_bit) * rank_size),
                (1, rank_size, rank_size),
            )[0]
            term = jnp.einsum(
                "vr,sr->vs",
                window[code_row, code_col],
                coupling_block,
                preferred_element_type=jnp.float32,
            )
            summed = summed + member[code_row * 6 + code_col] * term
    return summed


def halo_coeffs(coeffs):
    grid_rows, grid_cols, vectors, rank_size = coeffs.shape
    flattened = coeffs.reshape(grid_rows, grid_cols, vectors * rank_size)
    padded = extended(flattened, ((GX, 0), (GY, 1)), 2)
    return padded.reshape(grid_rows + 4, grid_cols + 4, vectors, rank_size)


def shards(
    samples,
    leaf_basis,
    transfer,
    coupling,
    near_tiles,
    codes_local,
    counts_local,
    codes_upper,
    counts_upper,
):
    patch_size = samples.shape[0]
    vectors = samples.shape[2]
    rank_size = leaf_basis.shape[0]
    levels_local = transfer.shape[0] - 1
    images = []
    wide_samples = extended(samples, ((GX, 0), (GY, 1)), 2)
    first_padded = project(wide_samples, leaf_basis)
    leaf_coeffs = first_padded[2:-2, 2:-2]
    rim_samples = wide_samples[1:-1, 1:-1]
    coeffs = leaf_coeffs
    for level_index in range(levels_local):
        stride = 2**level_index
        member = member_table(
            codes_local[::stride, ::stride, level_index],
            counts_local[::stride, ::stride, level_index],
        )
        if level_index == 0 and first_padded is not None:
            padded = first_padded
        else:
            padded = halo_coeffs(coeffs)
        images.append(couple(padded, member, coupling[level_index]))
        coeffs = lift_level(coeffs, transfer[level_index])
    flat_block = coeffs.reshape(1, vectors * rank_size)
    everything = gathered_by_axis(flat_block, GX_GY, (0, 2, 3, 1), 0)
    block_grid = everything.reshape(lax.axis_size(GX), lax.axis_size(GY), vectors, rank_size)
    upper_coeffs = [block_grid]
    while upper_coeffs[-1].shape[0] > 2:
        upper_coeffs.append(lift_level(upper_coeffs[-1], transfer[levels_local]))
    row_index = lax.axis_index(GX)
    col_index = lax.axis_index(GY)
    offset = 0
    upper_images = []
    for upper_step, coeffs_here in enumerate(upper_coeffs):
        grid_cols = coeffs_here.shape[1]
        row_here = row_index // 2**upper_step
        col_here = col_index // 2**upper_step
        index_here = offset + row_here * grid_cols + col_here
        list_row = lax.dynamic_slice_in_dim(codes_upper, index_here, 1, 0)
        count_row = lax.dynamic_slice_in_dim(counts_upper, index_here, 1, 0)
        member = member_table(list_row, count_row)[0]
        padded = jnp.pad(coeffs_here, ((2, 2), (2, 2), (0, 0), (0, 0)))
        upper_images.append(couple_one(padded, member, coupling[levels_local], row_here, col_here))
        offset = offset + coeffs_here.shape[0] * grid_cols
    downward = upper_images[-1]
    for upper_step in range(len(upper_coeffs) - 2, -1, -1):
        row_here = row_index // 2**upper_step
        col_here = col_index // 2**upper_step
        child_slot = row_here % 2 * 2 + col_here % 2
        carried = jnp.einsum(
            "vs,sc->vc",
            downward.astype(jnp.bfloat16),
            transfer[levels_local],
            preferred_element_type=jnp.float32,
        )
        downward = upper_images[upper_step] + lax.dynamic_slice_in_dim(
            carried, child_slot * rank_size, rank_size, 1
        )
    downward = downward[None, None]
    for level_index in range(levels_local - 1, -1, -1):
        downward = images[level_index] + spread(
            downward.astype(jnp.bfloat16), transfer[level_index]
        )
    summed = jnp.einsum(
        "ijvr,rs->ijvs",
        downward.astype(jnp.bfloat16),
        leaf_basis,
        preferred_element_type=jnp.float32,
    )
    for step_row in range(3):
        for step_col in range(3):
            neighbour = rim_samples[
                step_row : step_row + patch_size, step_col : step_col + patch_size
            ]
            summed = summed + jnp.einsum(
                "ijvs,ts->ijvt",
                neighbour,
                near_tiles[step_row * 3 + step_col],
                preferred_element_type=jnp.float32,
            )
    return summed.astype(jnp.bfloat16)


def solution(mesh):
    torus = Mesh(mesh.devices.reshape(4, 2, 4, 4), ("gx_0", "gx_1", "gy_0", "gy_1"))
    in_specs = (
        P(GX, GY, None, None),
        P(),
        P(),
        P(),
        P(),
        P(GX, GY, None, None),
        P(GX, GY, None),
        P(),
        P(),
    )
    out_specs = P(GX, GY, None, None)
    return jax.shard_map(
        shards, mesh=torus, in_specs=in_specs, out_specs=out_specs, check_vma=False
    )
```

profile of v0, /device:TPU:38, one launch (start us, length us, event | category | flops | bytes accessed | tf_op | source)
XLA Modules:
  0.0 625.4 jit_solution(9527153466392710589)
XLA Ops:
  41.1 5.5 fusion.17
  78.8 6.7 %fusion.435 = f32[16,16,32,256]{3,2,1,0:T(8,128)} fusion(bf16[16,16,32,256]{3,2,1,0:T(8,128)(2,1)} %param.9, bf16[9,256,256]{2,1,0:T(8,128)(2,1)} %param.13), kind=kOutput, calls=%fused_computation.926 | convolution fusion | flops 1073741824 | bytes 12713984 | tf_op jit(solution)/shard_map/ijvs,ts->ijvt/dot_general | solution.py:248
  100.2 5.4 fusion.10
  105.6 5.4 fusion.6
  111.2 6.2 collective-permute-done.2
  130.1 12.0 %all_gather.12 = bf16[4,1,2048]{2,1,0:T(2,128)(2,1)S(1)} all-gather(bf16[1,1,2048]{2,1,0:T(2,128)(2,1)S(1)} %broadcast_in_dim_reshape.3), channel_id=1, replica_groups=mesh['gx_0'=4,'gx_1'=2,'gy_0'=4,'gy_1'=4] {'gx_0'}, dimensions={0}, use_global_device_ids=true | all-gather | bytes 20480 | tf_op jit(solution)/shard_map/all_gather | solution.py:34
  142.1 13.2 %all_gather.13 = bf16[16,1,2048]{2,1,0:T(2,128)(2,1)S(1)} all-gather(bf16[4,1,2048]{2,1,0:T(2,128)(2,1)S(1)} %all_gather.12), channel_id=1, replica_groups=mesh['gx_0'=4,'gx_1'=2,'gy_0'=4,'gy_1'=4] {'gy_0'}, dimensions={0}, use_global_device_ids=true | all-gather | bytes 81920 | tf_op jit(solution)/shard_map/all_gather | solution.py:34
  155.3 12.3 %all_gather.14 = bf16[64,1,2048]{2,0,1:T(8,128)(2,1)S(1)} all-gather(bf16[16,1,2048]{2,0,1:T(8,128)(2,1)S(1)} %copy.124), channel_id=1, replica_groups=mesh['gx_0'=4,'gx_1'=2,'gy_0'=4,'gy_1'=4] {'gy_1'}, dimensions={0}, use_global_device_ids=true | all-gather | bytes 327680 | tf_op jit(solution)/shard_map/all_gather | solution.py:34
  341.3 15.0 %fusion.148 = f32[1,8,8,32,64]{4,3,2,1,0:T(8,128)} fusion(f32[8,8,32,256]{3,2,1,0:T(8,128)} %fusion.267, f32[8,8,32,256]{3,2,1,0:T(8,128)S(1)} %fusion.269, f32[8,8,32,256]{3,2,1,0:T(8,128)} %fusion.271, f32[8,8,32,256]{3,2,1,0:T(8,128)} %fusion.273, f32[8,8,32,256]{3,2,1,0:T(8,128)} %fusion.275, f32[8,8,32,256]{3,2,1,0:T(8,128)} %fusion.277, ...), kind=kLoop, calls=%fused_computation.411 | loop fusion | flops 6946816 | bytes 14686976 | tf_op jit(solution)/shard_map/stack | solution.py:127
  359.0 8.8 %fusion.175 = f32[1,8,8,32,64]{4,3,2,1,0:T(8,128)} fusion(f32[8,8,32,256]{3,2,1,0:T(8,128)S(1)} %copy-done.18, f32[8,8,32,256]{3,2,1,0:T(8,128)S(1)} %fusion.269, f32[8,8,32,256]{3,2,1,0:T(8,128)S(1)} %copy-done.5, f32[8,8,32,256]{3,2,1,0:T(8,128)S(1)} %copy-done.6, f32[8,8,32,256]{3,2,1,0:T(8,128)S(1)} %copy-done.7, f32[8,8,32,256]{3,2,1,0:T(8,128)S(1)} %copy-done.8, ...), kind=kLoop, calls=%fused_computation.465 | loop fusion | flops 6946816 | bytes 14686976 | tf_op jit(solution)/shard_map/stack | solution.py:127
  368.2 12.3 %fusion.202 = f32[1,8,8,32,64]{4,3,2,1,0:T(8,128)} fusion(f32[8,8,32,256]{3,2,1,0:T(8,128)S(1)} %copy-done.18, f32[8,8,32,256]{3,2,1,0:T(8,128)S(1)} %fusion.269, f32[8,8,32,256]{3,2,1,0:T(8,128)S(1)} %copy-done.5, f32[8,8,32,256]{3,2,1,0:T(8,128)S(1)} %copy-done.6, f32[8,8,32,256]{3,2,1,0:T(8,128)S(1)} %copy-done.7, f32[8,8,32,256]{3,2,1,0:T(8,128)S(1)} %copy-done.8, ...), kind=kLoop, calls=%fused_computation.519 | loop fusion | flops 6946816 | bytes 14686976 | tf_op jit(solution)/shard_map/stack | solution.py:127
  380.8 6.4 %fusion.229 = f32[1,8,8,32,64]{4,3,2,1,0:T(8,128)} fusion(f32[8,8,32,256]{3,2,1,0:T(8,128)S(1)} %copy-done.18, f32[8,8,32,256]{3,2,1,0:T(8,128)S(1)} %fusion.269, f32[8,8,32,256]{3,2,1,0:T(8,128)S(1)} %copy-done.5, f32[8,8,32,256]{3,2,1,0:T(8,128)S(1)} %copy-done.6, f32[8,8,32,256]{3,2,1,0:T(8,128)S(1)} %copy-done.7, f32[8,8,32,256]{3,2,1,0:T(8,128)S(1)} %copy-done.8, ...), kind=kLoop, calls=%fused_computation.573 | loop fusion | flops 6946816 | bytes 14686976 | tf_op jit(solution)/shard_map/stack | solution.py:127
  393.2 6.8 %fusion.25 = f32[16,16,32,256]{3,2,1,0:T(8,128)} fusion(bf16[20,16,32,256]{3,2,1,0:T(8,128)(2,1)} %copy-done.1, bf16[20,2,32,256]{3,2,1,0:T(8,128)(2,1)} %copy-done.28, bf16[9,256,256]{2,1,0:T(8,128)(2,1)} %param.13), kind=kOutput, calls=%fused_computation.138 | convolution fusion | flops 1085538304 | bytes 14417920 | tf_op jit(solution)/shard_map/ijvs,ts->ijvt/dot_general | solution.py:248
  400.0 6.7 %fusion.24 = f32[16,16,32,256]{3,2,1,0:T(8,128)} fusion(bf16[20,16,32,256]{3,2,1,0:T(8,128)(2,1)} %copy-done.1, bf16[20,2,32,256]{3,2,1,0:T(8,128)(2,1)S(1)} %copy-done.29, bf16[9,256,256]{2,1,0:T(8,128)(2,1)} %param.13), kind=kOutput, calls=%fused_computation.137 | convolution fusion | flops 1085538304 | bytes 14417920 | tf_op jit(solution)/shard_map/ijvs,ts->ijvt/dot_general | solution.py:248
  406.7 5.5 fusion.26
  412.2 5.4 fusion.22
  417.5 5.4 fusion.23
  447.9 6.0 collective-permute-start.11
  458.5 6.2 collective-permute-start.7
  474.9 17.4 %fusion.1578 = f32[1,1,1,32,64]{4,3,0,2,1:T(8,128)S(1)} fusion(f32[1,1,32,256]{3,2,1,0:T(8,128)S(1)} %convolution_bitcast_fusion.4, f32[1,1,32,256]{3,2,1,0:T(8,128)S(1)} %convolution_bitcast_fusion.5, f32[1,1,32,256]{3,2,1,0:T(8,128)S(1)} %convolution_bitcast_fusion.6, f32[1,1,32,256]{3,2,1,0:T(8,128)S(1)} %convolution_bitcast_fusion.7, ...), kind=kLoop, calls=%fused_computation.2436 | loop fusion | flops 108544 | bytes 229484 | tf_op jit(solution)/shard_map/stack | solution.py:127
  492.3 17.0 %fusion.1605 = f32[1,1,1,32,64]{4,3,0,2,1:T(8,128)S(1)} fusion(f32[1,1,32,256]{3,2,1,0:T(8,128)S(1)} %convolution_bitcast_fusion.4, f32[1,1,32,256]{3,2,1,0:T(8,128)S(1)} %convolution_bitcast_fusion.5, f32[1,1,32,256]{3,2,1,0:T(8,128)S(1)} %convolution_bitcast_fusion.6, f32[1,1,32,256]{3,2,1,0:T(8,128)S(1)} %convolution_bitcast_fusion.7, ...), kind=kLoop, calls=%fused_computation.2490 | loop fusion | flops 108544 | bytes 229484 | tf_op jit(solution)/shard_map/stack | solution.py:127
  509.9 16.7 %fusion.1551 = f32[1,1,1,32,64]{4,3,2,1,0:T(8,128)S(1)} fusion(f32[1,1,32,256]{3,2,1,0:T(8,128)S(1)} %convolution_bitcast_fusion.4, f32[1,1,32,256]{3,2,1,0:T(8,128)S(1)} %convolution_bitcast_fusion.5, f32[1,1,32,256]{3,2,1,0:T(8,128)S(1)} %convolution_bitcast_fusion.6, f32[1,1,32,256]{3,2,1,0:T(8,128)S(1)} %convolution_bitcast_fusion.7, ...), kind=kLoop, calls=%fused_computation.2382 | loop fusion | flops 108544 | bytes 229484 | tf_op jit(solution)/shard_map/stack | solution.py:127
  526.7 17.0 %fusion.1524 = f32[1,1,1,32,64]{4,3,2,1,0:T(8,128)S(1)} fusion(f32[1,1,32,256]{3,2,1,0:T(8,128)S(1)} %convolution_bitcast_fusion.4, f32[1,1,32,256]{3,2,1,0:T(8,128)S(1)} %convolution_bitcast_fusion.5, f32[1,1,32,256]{3,2,1,0:T(8,128)S(1)} %convolution_bitcast_fusion.6, f32[1,1,32,256]{3,2,1,0:T(8,128)S(1)} %convolution_bitcast_fusion.7, ...), kind=kLoop, calls=%fused_computation.2328 | loop fusion | flops 108544 | bytes 229484 | tf_op jit(solution)/shard_map/stack | solution.py:127
  598.7 26.5 %add_convert_fusion = bf16[16,16,32,256]{3,2,1,0:T(8,128)(2,1)} fusion(f32[16,16,32,256]{3,2,1,0:T(8,128)} %fusion.10, f32[16,16,32,256]{3,2,1,0:T(8,128)} %fusion.24, f32[16,16,32,256]{3,2,1,0:T(8,128)} %fusion.22, f32[16,16,32,256]{3,2,1,0:T(8,128)} %fusion.435, f32[16,16,32,256]{3,2,1,0:T(8,128)} %fusion.25, f32[16,16,32,256]{3,2,1,0:T(8,128)} %fusion.23, ...), kind=kOutput, calls=%fused_computation.36 | convolution fusion | flops 1106509824 | bytes 85721088 | tf_op jit(solution)/shard_map/ijvs,ts->ijvt/dot_general | solution.py:248
  (1187 shorter events, 373.1 us)
Async XLA Ops:
  0.0 117.4 %copy-start = (bf16[64,256]{1,0:T(8,128)(2,1)S(1)}, bf16[64,256]{1,0:T(8,128)(2,1)}, u32[]{:S(2)}) copy-start(bf16[64,256]{1,0:T(8,128)(2,1)} %param.10) | copy-start | bytes 98308
  2.3 88.2 %collective-permute-start = (bf16[2,16,32,256]{3,2,1,0:T(8,128)(2,1)}, bf16[2,16,32,256]{3,2,1,0:T(8,128)(2,1)S(1)}, u32[]{:S(2)}, u32[]{:S(2)}) collective-permute-start(bf16[2,16,32,256]{3,2,1,0:T(8,128)(2,1)} %get-tuple-element.334), channel_id=1, source_target_pairs={{0,16},{16,32},{32,48},{48,64},{64,80},{80,96},{96,112},{1,17},{17... | collective-permute-start | bytes 1572872 | tf_op jit(solution)/shard_map/ppermute | solution.py:17
  4.4 89.2 %collective-permute-start.1 = (bf16[2,16,32,256]{3,2,1,0:T(8,128)(2,1)}, bf16[2,16,32,256]{3,2,1,0:T(8,128)(2,1)S(1)}, u32[]{:S(2)}, u32[]{:S(2)}) collective-permute-start(bf16[2,16,32,256]{3,2,1,0:T(8,128)(2,1)} %get-tuple-element.335), channel_id=1, source_target_pairs={{16,0},{32,16},{48,32},{64,48},{80,64},{96,80},{112,96},{17,1},{33... | collective-permute-start | bytes 1572872 | tf_op jit(solution)/shard_map/ppermute | solution.py:20
  93.7 17.4 %collective-permute-start.3 = (bf16[20,2,32,256]{3,2,1,0:T(8,128)(2,1)S(1)}, bf16[20,2,32,256]{3,2,1,0:T(8,128)(2,1)S(1)}, u32[]{:S(2)}, u32[]{:S(2)}) collective-permute-start(bf16[20,2,32,256]{3,2,1,0:T(8,128)(2,1)S(1)} %get-tuple-element.332), channel_id=1, source_target_pairs={{1,0},{2,1},{3,2},{4,3},{5,4},{6,5},{7,6},{8,7},{9,8},{10,9},{11,1... | collective-permute-start | bytes 1966088 | tf_op jit(solution)/shard_map/ppermute | solution.py:20
  98.2 19.2 %collective-permute-start.2 = (bf16[20,2,32,256]{3,2,1,0:T(8,128)(2,1)S(1)}, bf16[20,2,32,256]{3,2,1,0:T(8,128)(2,1)S(1)}, u32[]{:S(2)}, u32[]{:S(2)}) collective-permute-start(bf16[20,2,32,256]{3,2,1,0:T(8,128)(2,1)S(1)} %get-tuple-element.333), channel_id=1, source_target_pairs={{0,1},{1,2},{2,3},{3,4},{4,5},{5,6},{6,7},{7,8},{8,9},{9,10},{10,1... | collective-permute-start | bytes 1966088 | tf_op jit(solution)/shard_map/ppermute | solution.py:17
  230.5 217.3 %collective-permute-start.4 = (bf16[2,8,2048]{2,1,0:T(8,128)(2,1)}, bf16[2,8,2048]{2,1,0:T(8,128)(2,1)}, u32[]{:S(2)}, u32[]{:S(2)}) collective-permute-start(bf16[2,8,2048]{2,1,0:T(8,128)(2,1)} %slice.5004), channel_id=1, source_target_pairs={{0,16},{16,32},{32,48},{48,64},{64,80},{80,96},{96,112},{1,17},{17... | collective-permute-start | bytes 196616 | tf_op jit(solution)/shard_map/ppermute | solution.py:17
  232.6 200.8 %collective-permute-start.12 = (bf16[2,2,2048]{2,1,0:T(2,128)(2,1)}, bf16[2,2,2048]{2,1,0:T(2,128)(2,1)}, u32[]{:S(2)}, u32[]{:S(2)}) collective-permute-start(bf16[2,2,2048]{2,1,0:T(2,128)(2,1)} %reshape.1625), channel_id=1, source_target_pairs={{0,16},{16,32},{32,48},{48,64},{64,80},{80,96},{96,112},{1,17},{17... | collective-permute-start | bytes 49160 | tf_op jit(solution)/shard_map/ppermute | solution.py:17
  235.2 205.2 %collective-permute-start.8 = (bf16[2,4,2048]{2,1,0:T(4,128)(2,1)}, bf16[2,4,2048]{2,1,0:T(4,128)(2,1)}, u32[]{:S(2)}, u32[]{:S(2)}) collective-permute-start(bf16[2,4,2048]{2,1,0:T(4,128)(2,1)} %slice.5302), channel_id=1, source_target_pairs={{0,16},{16,32},{32,48},{48,64},{64,80},{80,96},{96,112},{1,17},{17... | collective-permute-start | bytes 98312 | tf_op jit(solution)/shard_map/ppermute | solution.py:17
  426.7 11.7 %collective-permute-start.13 = (bf16[2,2,2048]{2,1,0:T(2,128)(2,1)}, bf16[2,2,2048]{2,1,0:T(2,128)(2,1)S(1)}, u32[]{:S(2)}, u32[]{:S(2)}) collective-permute-start(bf16[2,2,2048]{2,1,0:T(2,128)(2,1)} %reshape.1625), channel_id=1, source_target_pairs={{16,0},{32,16},{48,32},{64,48},{80,64},{96,80},{112,96},{17,1},{33... | collective-permute-start | bytes 49160 | tf_op jit(solution)/shard_map/ppermute | solution.py:20
  430.8 24.1 %collective-permute-start.5 = (bf16[2,8,2048]{2,1,0:T(8,128)(2,1)S(1)}, bf16[2,8,2048]{2,1,0:T(8,128)(2,1)S(1)}, u32[]{:S(2)}, u32[]{:S(2)}) collective-permute-start(bf16[2,8,2048]{2,1,0:T(8,128)(2,1)S(1)} %slice.5006), channel_id=1, source_target_pairs={{16,0},{32,16},{48,32},{64,48},{80,64},{96,80},{112,96},{17,1},{33... | collective-permute-start | bytes 196616 | tf_op jit(solution)/shard_map/ppermute | solution.py:20
  433.4 11.7 %collective-permute-start.9 = (bf16[2,4,2048]{2,1,0:T(4,128)(2,1)S(1)}, bf16[2,4,2048]{2,1,0:T(4,128)(2,1)S(1)}, u32[]{:S(2)}, u32[]{:S(2)}) collective-permute-start(bf16[2,4,2048]{2,1,0:T(4,128)(2,1)S(1)} %slice.5304), channel_id=1, source_target_pairs={{16,0},{32,16},{48,32},{64,48},{80,64},{96,80},{112,96},{17,1},{33... | collective-permute-start | bytes 98312 | tf_op jit(solution)/shard_map/ppermute | solution.py:20
  438.5 20.0 %collective-permute-start.15 = (bf16[6,2,2048]{2,1,0:T(2,128)(2,1)S(1)}, bf16[6,2,2048]{2,1,0:T(2,128)(2,1)S(1)}, u32[]{:S(2)}, u32[]{:S(2)}) collective-permute-start(bf16[6,2,2048]{2,1,0:T(2,128)(2,1)S(1)} %constant_dynamic-update-slice_fusion.9), channel_id=1, source_target_pairs={{1,0},{2,1},{3,2},{4,3},{5,4},{6,5},{7,6},{8,7},{9,8},{10,9},{11,1... | collective-permute-start | bytes 147464 | tf_op jit(solution)/shard_map/ppermute | solution.py:20
  440.4 24.3 %collective-permute-start.14 = (bf16[6,2,2048]{2,1,0:T(2,128)(2,1)S(1)}, bf16[6,2,2048]{2,1,0:T(2,128)(2,1)S(1)}, u32[]{:S(2)}, u32[]{:S(2)}) collective-permute-start(bf16[6,2,2048]{2,1,0:T(2,128)(2,1)S(1)} %constant_dynamic-update-slice_fusion.9), channel_id=1, source_target_pairs={{0,1},{1,2},{2,3},{3,4},{4,5},{5,6},{6,7},{7,8},{8,9},{9,10},{10,1... | collective-permute-start | bytes 147464 | tf_op jit(solution)/shard_map/ppermute | solution.py:17
  446.0 98.3 %collective-permute-start.10 = (bf16[8,2,2048]{2,1,0:T(2,128)(2,1)}, bf16[8,2,2048]{2,1,0:T(2,128)(2,1)}, u32[]{:S(2)}, u32[]{:S(2)}) collective-permute-start(bf16[8,2,2048]{2,1,0:T(2,128)(2,1)} %get-tuple-element.509), channel_id=1, source_target_pairs={{0,1},{1,2},{2,3},{3,4},{4,5},{5,6},{6,7},{7,8},{8,9},{9,10},{10,1... | collective-permute-start | bytes 196616 | tf_op jit(solution)/shard_map/ppermute | solution.py:17
  447.9 96.4 %collective-permute-start.11 = (bf16[8,2,2048]{2,1,0:T(2,128)(2,1)}, bf16[8,2,2048]{2,1,0:T(2,128)(2,1)}, u32[]{:S(2)}, u32[]{:S(2)}) collective-permute-start(bf16[8,2,2048]{2,1,0:T(2,128)(2,1)} %get-tuple-element.510), channel_id=1, source_target_pairs={{1,0},{2,1},{3,2},{4,3},{5,4},{6,5},{7,6},{8,7},{9,8},{10,9},{11,1... | collective-permute-start | bytes 196616 | tf_op jit(solution)/shard_map/ppermute | solution.py:20
  456.5 106.2 %collective-permute-start.6 = (bf16[12,2,2048]{2,1,0:T(2,128)(2,1)}, bf16[12,2,2048]{2,1,0:T(2,128)(2,1)}, u32[]{:S(2)}, u32[]{:S(2)}) collective-permute-start(bf16[12,2,2048]{2,1,0:T(2,128)(2,1)} %get-tuple-element.503), channel_id=1, source_target_pairs={{0,1},{1,2},{2,3},{3,4},{4,5},{5,6},{6,7},{7,8},{8,9},{9,10},{10,1... | collective-permute-start | bytes 294920 | tf_op jit(solution)/shard_map/ppermute | solution.py:17
  458.5 104.1 %collective-permute-start.7 = (bf16[12,2,2048]{2,1,0:T(2,128)(2,1)}, bf16[12,2,2048]{2,1,0:T(2,128)(2,1)}, u32[]{:S(2)}, u32[]{:S(2)}) collective-permute-start(bf16[12,2,2048]{2,1,0:T(2,128)(2,1)} %get-tuple-element.504), channel_id=1, source_target_pairs={{1,0},{2,1},{3,2},{4,3},{5,4},{6,5},{7,6},{8,7},{9,8},{10,9},{11,1... | collective-permute-start | bytes 294920 | tf_op jit(solution)/shard_map/ppermute | solution.py:20
  474.7 71.5 %copy-start.69 = (bf16[64,64]{0,1:T(8,128)(2,1)S(1)}, bf16[64,64]{0,1:T(8,128)(2,1)}, u32[]{:S(2)}) copy-start(bf16[64,64]{0,1:T(8,128)(2,1)} %get-tuple-element.418) | copy-start | bytes 24580
  474.7 71.7 %copy-start.73 = (bf16[64,64]{0,1:T(8,128)(2,1)S(1)}, bf16[64,64]{0,1:T(8,128)(2,1)}, u32[]{:S(2)}) copy-start(bf16[64,64]{0,1:T(8,128)(2,1)} %get-tuple-element.404) | copy-start | bytes 24580
  474.7 71.7 %copy-start.76 = (bf16[64,64]{0,1:T(8,128)(2,1)S(1)}, bf16[64,64]{0,1:T(8,128)(2,1)}, u32[]{:S(2)}) copy-start(bf16[64,64]{0,1:T(8,128)(2,1)} %get-tuple-element.399) | copy-start | bytes 24580
  474.8 71.8 %copy-start.71 = (bf16[64,64]{0,1:T(8,128)(2,1)S(1)}, bf16[64,64]{0,1:T(8,128)(2,1)}, u32[]{:S(2)}) copy-start(bf16[64,64]{0,1:T(8,128)(2,1)} %get-tuple-element.408) | copy-start | bytes 24580
  474.8 72.0 %copy-start.78 = (bf16[64,64]{0,1:T(8,128)(2,1)S(1)}, bf16[64,64]{0,1:T(8,128)(2,1)}, u32[]{:S(2)}) copy-start(bf16[64,64]{0,1:T(8,128)(2,1)} %get-tuple-element.392) | copy-start | bytes 24580
  474.8 72.0 %copy-start.79 = (bf16[64,64]{0,1:T(8,128)(2,1)S(1)}, bf16[64,64]{0,1:T(8,128)(2,1)}, u32[]{:S(2)}) copy-start(bf16[64,64]{0,1:T(8,128)(2,1)} %get-tuple-element.391) | copy-start | bytes 24580
  474.8 72.2 %copy-start.77 = (bf16[64,64]{0,1:T(8,128)(2,1)S(1)}, bf16[64,64]{0,1:T(8,128)(2,1)}, u32[]{:S(2)}) copy-start(bf16[64,64]{0,1:T(8,128)(2,1)} %get-tuple-element.393) | copy-start | bytes 24580
  (372 other events, 3471.4 us)
where the time goes:
time: 637 us; the launch traced here: 625 us
  matrix products  268 us (42%)
  other arithmetic  143 us (22%)
  local copies, waits for them, and re-layouts  112 us (18%)
  starting transfers between devices  49.8 us (8%)
  blocking collectives  39.7 us (6%)
  between operations  6.47 us (1%)
  waiting for transfers between devices  6.44 us (1%)
    another operation x16, other arithmetic, couple(): jnp.stack(totals[row_bit], axis=0)  125 us
    dot_general x106, matrix products, couple_one(): jnp.einsum('vr,sr->vs', window[code_row, code_col], coupling_block, prefe...  92.1 us
    dot_general x128, matrix products, couple(): jnp.einsum('pqvr,sr->pqvs', source, blocks, preferred_element_type=jnp.fl...  86.4 us
    dot_general x9, matrix products, shards(): jnp.einsum('ijvs,ts->ijvt', neighbour, near_tiles[step_row * 3 + step_col...  73.8 us
    all_gather x4, blocking collectives, stacked_from(): blocks = lax.all_gather(blocks, axes[k], axis=0, tiled=True)  39.7 us
    slice x24, local copies, waits for them, and re-layouts, couple(): weight_mask = member[:, row_bit, :, col_bit, code_row * 6 + code_col]  39.4 us
    ppermute x8, starting transfers between devices, extended(): lax.ppermute(lax.slice_in_dim(block, 0, width, axis=dim), axis, backward)  32.1 us
    ppermute x8, starting transfers between devices, extended(): lax.ppermute(lax.slice_in_dim(block, block.shape[dim] - width, None, axis...  17.7 us
  transfers between devices with their start and end apart: 16, of which 2 were waited for; matrix products, arithmetic and copies ran while one was open for 61% of the time, Pallas kernels for 0%

commit v1 on v0

v1 whole, which is shorter than its diff:
```python
import jax
import jax.numpy as jnp
from jax import lax
from jax.experimental import pallas as pl
from jax.experimental.pallas import tpu as pltpu
from jax.sharding import PartitionSpec as P


BF = jnp.bfloat16
F32 = jnp.float32
RANK = 64
VEC = 32
VMEM = pltpu.VMEM


def dot_nt(a, b):
    return lax.dot_general(a, b, (((1,), (1,)), ((), ())), preferred_element_type=F32)


def dot_nn(a, b):
    return lax.dot_general(a, b, (((1,), (0,)), ((), ())), preferred_element_type=F32)


def pair_rhs(matrix):
    zeros = jnp.zeros_like(matrix)
    return jnp.concatenate(
        [jnp.concatenate([matrix, zeros], 0), jnp.concatenate([zeros, matrix], 0)], 1
    )


def split_pairs(value):
    n, vec, k = value.shape
    v = value.reshape(n // 2, 2, vec, k)
    return jnp.concatenate(
        [v[:, 0].reshape(n // 2 * vec, k), v[:, 1].reshape(n // 2 * vec, k)], 1
    )


def lift_rows(upper, lower, rhs):
    both = jnp.concatenate([upper, lower], 2)
    out = dot_nt(split_pairs(both), rhs)
    return out.astype(BF).reshape(upper.shape[0] // 2, VEC, 128)


EDGE = 10


def gx_units(q_sizes, patch):
    def edge(last):
        units = []
        for level, n in enumerate(q_sizes):
            for row in range(2):
                units.append(("q", level, row, (n // 2 - 1) if last else 0))
        for half in range(2):
            units.append(("s", patch - 1 if last else 0, half))
        return units

    left, right = edge(False), edge(True)
    middle = []
    for level, n in enumerate(q_sizes):
        for row in range(2):
            for p in range(1, n // 2 - 1):
                middle.append(("q", level, row, p))
    for cell in range(1, patch - 1):
        for half in range(2):
            middle.append(("s", cell, half))
    return left + middle + right


def gy_starts(q_sizes, patch):
    starts = []
    at = 0
    for n in q_sizes:
        starts.append(at)
        at += n
    return starts, at, at + 2 * patch


def project_kernel(hbm_ref, basis_ref, transfer_ref, *refs):
    outs, bufs, (s_ref, sems, row_sems, out_sems) = refs[:9], refs[9:18], refs[18:]
    q0, q1, q2, q3, q4, gx_lo, gx_hi, gy_left, gy_right = bufs
    patch = s_ref.shape[0]
    qs = [q0, q1, q2, q3]
    sizes = [q.shape[0] for q in qs]

    def copy(i):
        return pltpu.make_async_copy(hbm_ref.at[i], s_ref.at[i], sems.at[i])

    def put_row(i):
        return pltpu.make_async_copy(q0.at[i], outs[0].at[i], row_sems.at[i])

    def put(k):
        return pltpu.make_async_copy(bufs[k], outs[k], out_sems.at[k])

    def fetch(i, carry):
        copy(i).start()
        return carry

    lax.fori_loop(0, patch, fetch, 0)
    basis = pair_rhs(basis_ref[...])
    starts, base, _ = gy_starts(sizes, patch)

    def row(i, carry):
        copy(i).wait()
        q0[i] = dot_nt(split_pairs(s_ref[i]), basis).astype(BF).reshape(patch // 2, VEC, 128)
        put_row(i).start()
        for half in range(2):
            cols = slice(half * 128, half * 128 + 128)
            gy_left[EDGE + base + 2 * i + half] = s_ref[i, 0, :, cols]
            gy_right[EDGE + base + 2 * i + half] = s_ref[i, patch - 1, :, cols]
        return carry

    lax.fori_loop(0, patch, row, 0)
    for level in range(3):
        rhs = pair_rhs(transfer_ref[level])
        for r in range(sizes[level + 1]):
            qs[level + 1][r] = lift_rows(qs[level][2 * r], qs[level][2 * r + 1], rhs)
        put(level + 1).start()
    for number, unit in enumerate(gx_units(sizes, patch)):
        if unit[0] == "q":
            _, level, r, p = unit
            gx_lo[number] = qs[level][r, p]
            gx_hi[number] = qs[level][sizes[level] - 2 + r, p]
        else:
            _, cell, half = unit
            gx_lo[number] = s_ref[0, cell, :, half * 128 : half * 128 + 128]
            gx_hi[number] = s_ref[patch - 1, cell, :, half * 128 : half * 128 + 128]
    put(5).start()
    put(6).start()
    both = jnp.concatenate([q3[0, 0], q3[1, 0]], 1)
    both = jnp.concatenate([both[: VEC // 2], both[VEC // 2 :]], 1)
    top = dot_nt(both, pair_rhs(transfer_ref[3])).astype(BF)
    q4[...] = jnp.broadcast_to(top[None], q4.shape)
    put(4).start()
    zeros = jnp.zeros((EDGE, VEC, 128), BF)
    for ref in (gy_left, gy_right):
        ref[0:EDGE] = zeros
        ref[ref.shape[0] - EDGE : ref.shape[0]] = zeros
    for level in range(4):
        n = sizes[level]
        at = EDGE + starts[level]
        gy_left[at : at + n] = qs[level][:, 0]
        gy_right[at : at + n] = qs[level][:, n // 2 - 1]
    put(7).start()
    put(8).start()

    def wait_row(i, carry):
        put_row(i).wait()
        return carry

    lax.fori_loop(0, patch, wait_row, 0)
    for k in range(1, 9):
        put(k).wait()


def corner_kernel(from_lo, from_hi, left_in, right_in, left, right, buf, sems):
    del left_in, right_in
    n = left.shape[0]
    m = from_lo.shape[0]
    moves = [
        (from_lo.at[0:EDGE], left.at[0:EDGE]),
        (from_hi.at[0:EDGE], left.at[n - EDGE : n]),
        (from_lo.at[m - EDGE : m], right.at[0:EDGE]),
        (from_hi.at[m - EDGE : m], right.at[n - EDGE : n]),
    ]
    gets = [pltpu.make_async_copy(a, buf.at[k], sems.at[k]) for k, (a, b) in enumerate(moves)]
    puts = [pltpu.make_async_copy(buf.at[k], b, sems.at[4 + k]) for k, (a, b) in enumerate(moves)]
    for get in gets:
        get.start()
    for get, put in zip(gets, puts):
        get.wait()
        put.start()
    for put in puts:
        put.wait()


def list_words(codes, counts):
    slot = lax.broadcasted_iota(jnp.int32, codes.shape, codes.ndim - 1)
    active = slot < counts
    words = []
    for group in range(2):
        here = active & ((codes >= 18) if group else (codes < 18))
        shift = jnp.where(here, codes - 18 * group, 0)
        power = jnp.where(here, lax.shift_left(jnp.ones_like(codes), shift), 0)
        words.append(power.astype(F32))
    return words


def word_offsets(sizes):
    offsets = [0]
    for n in sizes:
        offsets.append(offsets[-1] + n * n)
    return offsets


def near_kernel(
    s_hbm, tiles_hbm, codes_ref, counts_ref, acc_hbm, words_hbm,
    s_ref, acc_ref, w_ref, tiles_ref, words_ref, in_sems, out_sems, more_sems,
):
    patch = s_ref.shape[0]

    def fetch(i):
        return pltpu.make_async_copy(s_hbm.at[i], s_ref.at[i], in_sems.at[i])

    def put_out(k):
        rows = pl.ds(2 * k, 2)
        return pltpu.make_async_copy(acc_ref.at[rows], acc_hbm.at[rows], out_sems.at[k])

    def start_fetch(i, carry):
        fetch(i).start()
        return carry

    fetch_tiles = pltpu.make_async_copy(tiles_hbm, tiles_ref, more_sems.at[0])
    put_words = pltpu.make_async_copy(words_ref, words_hbm, more_sems.at[1])
    fetch_tiles.start()
    lax.fori_loop(0, patch, start_fetch, 0)
    levels = counts_ref.shape[1]
    at = 0
    for level in range(levels):
        n = patch >> level
        counts = counts_ref[:, level : level + 1]
        codes = codes_ref[:, level, :]
        for group, power in enumerate(list_words(codes, counts)):
            word = jnp.sum(power, axis=1, keepdims=True).astype(jnp.int32)
            word = jnp.broadcast_to(word, (patch * patch, 128))
            for i in range(n):
                for j in range(n):
                    r = ((i * patch + j) << level)
                    words_ref[at + i * n + j, group] = jnp.broadcast_to(word[r : r + 1], (8, 128))
        at += n * n
    put_words.start()
    fetch_tiles.wait()
    for k in range(9):
        w_ref[k * 256 : k * 256 + 256] = tiles_ref[k].T
    zeros = jnp.zeros((VEC, 256), BF)

    def shifted(value):
        return [
            jnp.concatenate([zeros, value[:-VEC]], 0),
            value,
            jnp.concatenate([value[VEC:], zeros], 0),
        ]

    def put(i, rows):
        blocks = [
            jnp.zeros((patch * VEC, 256), BF) if r is None else s_ref[r].reshape(patch * VEC, 256)
            for r in rows
        ]
        lhs = []
        for d in range(3):
            for upper, lower in zip(shifted(blocks[d]), shifted(blocks[d + 1])):
                lhs.append(jnp.concatenate([upper, lower], 0))
        out = dot_nn(jnp.concatenate(lhs, 1), w_ref[...])
        acc_ref[pl.ds(i, 2)] = out.reshape(2, patch, VEC, 256)

    for i in range(3):
        fetch(i).wait()
    put(0, [None, 0, 1, 2])
    put_out(0).start()

    def row(k, carry):
        i = 2 * k
        fetch(i + 1).wait()
        fetch(i + 2).wait()
        put(i, [i - 1, i, i + 1, i + 2])
        put_out(k).start()
        return carry

    lax.fori_loop(1, patch // 2 - 1, row, 0)
    fetch(patch - 1).wait()
    put(patch - 2, [patch - 3, patch - 2, patch - 1, None])
    put_out(patch // 2 - 1).start()

    def wait_out(k, carry):
        put_out(k).wait()
        return carry

    lax.fori_loop(0, patch // 2, wait_out, 0)
    put_words.wait()


def chunk_list(row_bit):
    chunks = []
    for a in range(6):
        for bp in range(3):
            if bp == 1 and 1 + row_bit <= a <= 3 + row_bit:
                continue
            chunks.append((a, bp))
    return chunks


def lane_bits():
    lane = lax.broadcasted_iota(jnp.int32, (8, 128), 1)
    return (lane >= 64).astype(jnp.int32)


def mask_of(words, a, bp, lanes):
    code = (a % 3) * 6 + 2 * bp
    bit = lax.shift_right_logical(words[a // 3], lanes + code) & 1
    m = bit.astype(F32)
    return jnp.concatenate([m, m, m, m], 0).astype(BF)


def final_kernel(
    counts_upper_ref, codes_upper_ref,
    *refs,
):
    n_in = 15
    sources, out_ref, buffers, rest = refs[:n_in], refs[n_in], refs[n_in + 1 : 2 * n_in + 1], refs[2 * n_in + 1 :]
    (
        transfer_ref, every, coupling_ref, words_ref, q0, q1, q2, q3,
        from_lo, from_hi, from_left, from_right, basis_ref, tiles_ref, acc_ref,
    ) = buffers
    (
    e0, e1, e2, e3, f4, f5, f6, shifted, b0, b1, b2, b3, cols, edge_col, edge_row, out_buf, sems, in_sems, acc_sems,
    ) = rest
    patch = acc_ref.shape[0]

    def fetch(k):
        return pltpu.make_async_copy(sources[k], buffers[k], in_sems.at[k])

    def fetch_acc(i):
        return pltpu.make_async_copy(sources[n_in - 1].at[i], acc_ref.at[i], acc_sems.at[i])

    for k in range(n_in - 1):
        fetch(k).start()

    def start_acc(i, carry):
        fetch_acc(i).start()
        return carry

    lax.fori_loop(0, patch, start_acc, 0)
    qs = [q0, q1, q2, q3]
    es = [e0, e1, e2, e3]
    sizes = [q.shape[0] for q in qs]
    lanes = lane_bits()
    word_at = word_offsets(sizes)

    for k in range(3):
        fetch(k).wait()
    for level in range(5):
        for d in range(7):
            shifted[level, d] = coupling_ref[level, d, :, 64:448]

    def block(level, col_bit, d, bp):
        if col_bit == 1:
            return coupling_ref[level, d, :, bp * 128 : bp * 128 + 128]
        return shifted[level, d, :, bp * 128 : bp * 128 + 128]

    f4[...] = jnp.zeros_like(f4)
    f5[...] = jnp.zeros_like(f5)
    f6[...] = jnp.zeros_like(f6)
    rows4 = f4.shape[0] - 4
    pairs4 = f4.shape[1] - 2
    low = lax.broadcasted_iota(jnp.int32, (pairs4, VEC // 2, 128), 2) < 64
    for r in range(rows4):
        v = every[2 * pairs4 * r : 2 * pairs4 * (r + 1)].astype(F32).reshape(pairs4, 2, VEC // 2, 128)
        even, odd = v[:, 0], v[:, 1]
        top = jnp.where(low, even, pltpu.roll(odd, 64, 2))
        bottom = jnp.where(low, pltpu.roll(even, 64, 2), odd)
        f4[r + 2, 1 : pairs4 + 1] = jnp.concatenate([top, bottom], 1).astype(BF)
    rhs4 = pair_rhs(transfer_ref[4])
    for child, parent in ((f4, f5), (f5, f6)):
        n_rows = parent.shape[0] - 4
        n_pairs = child.shape[1] - 2
        for r in range(n_rows):
            parent[r + 2, 1 : n_pairs // 2 + 1] = lift_rows(
                child[2 * r + 2, 1 : n_pairs + 1], child[2 * r + 3, 1 : n_pairs + 1], rhs4
            )
    row_index = lax.axis_index("gx")
    col_index = lax.axis_index("gy")
    upper_codes = codes_upper_ref[...]
    upper_slot = lax.broadcasted_iota(jnp.int32, upper_codes.shape, 0)
    upper_list = lax.broadcasted_iota(jnp.int32, upper_codes.shape, 1)

    def upper_words(index):
        count = jnp.where(upper_list == index, counts_upper_ref[index], 0)
        here = upper_slot < count
        words = []
        for group in range(2):
            mine = here & ((upper_codes >= 18) if group else (upper_codes < 18))
            shift = jnp.where(mine, upper_codes - 18 * group, 0)
            power = jnp.where(mine, lax.shift_left(jnp.ones_like(shift), shift), 0)
            total = jnp.sum(power.astype(F32), axis=0, keepdims=True)
            total = jnp.sum(total, axis=1, keepdims=True)
            words.append(jnp.broadcast_to(total, (8, 128)).astype(jnp.int32))
        return words

    uppers = []
    offset = 0
    for step, f in enumerate((f4, f5, f6)):
        r_here = lax.shift_right_logical(row_index, step)
        c_here = lax.shift_right_logical(col_index, step)
        n_cols = 2 * (f.shape[1] - 2)
        index = offset + r_here * n_cols + c_here
        offset += (f.shape[0] - 4) * n_cols
        words = upper_words(index)
        rb = r_here & 1
        cb = c_here & 1
        top_row = r_here - rb
        left = lax.shift_right_logical(c_here, 1)
        lhs, rhs = [], []
        for a in range(6):
            for bp in range(3):
                lhs.append(f[top_row + a, left + bp] * mask_of(words, a, bp, lanes))
            even = shifted[4, a + 1 - rb]
            odd = coupling_ref[4, a + 1 - rb][:, 0:384]
            rhs.append(jnp.where(cb == 1, odd, even))
        uppers.append(dot_nt(jnp.concatenate(lhs, 1), jnp.concatenate(rhs, 1)))
    down = uppers[-1]
    for step in (1, 0):
        r_here = lax.shift_right_logical(row_index, step)
        c_here = lax.shift_right_logical(col_index, step)
        carried = dot_nn(down.astype(BF), transfer_ref[4])
        half = jnp.where((r_here & 1) == 1, carried[:, 128:256], carried[:, 0:128])
        half = jnp.where((c_here & 1) == 1, pltpu.roll(half, 64, 1), half)
        down = uppers[step] + half[:, 0:64]
    carried3 = dot_nn(down.astype(BF), transfer_ref[3])

    for k in range(3, 12):
        fetch(k).wait()
    for level in range(4):
        n = sizes[level]
        es[level][2 : n + 2, 1 : n // 2 + 1] = qs[level][...]
    row_cells = {}
    for number, unit in enumerate(gx_units(sizes, patch)):
        if unit[0] == "q":
            _, level, r, p = unit
            es[level][r, p + 1] = from_lo[number]
            es[level][sizes[level] + 2 + r, p + 1] = from_hi[number]
        else:
            row_cells[unit[1:]] = number
    starts, base, total = gy_starts(sizes, patch)
    for side, ref in ((0, from_left), (1, from_right)):
        for level in range(4):
            n = sizes[level]
            p = 0 if side == 0 else n // 2 + 1
            es[level][0:2, p] = ref[2 * level : 2 * level + 2]
            es[level][2 : n + 2, p] = ref[EDGE + starts[level] : EDGE + starts[level] + n]
            hi = EDGE + total
            es[level][n + 2 : n + 4, p] = ref[hi + 2 * level : hi + 2 * level + 2]
        for half in range(2):
            c = slice(half * 128, half * 128 + 128)
            cols[side, 0, :, c] = ref[8 + half]
            cols[side, patch + 1, :, c] = ref[EDGE + total + 8 + half]
            for i in range(patch):
                cols[side, i + 1, :, c] = ref[EDGE + base + 2 * i + half]

    def images(level, group_rows, row_bit):
        n = sizes[level]
        e = es[level]
        out = []
        for col_bit in range(2):
            lhs, rhs = [], []
            words = []
            for group_row in group_rows:
                for group_col in range(n // 2):
                    at = word_at[level] + (2 * group_row + row_bit) * n + 2 * group_col + col_bit
                    words.append((words_ref[at, 0], words_ref[at, 1]))
            for a, bp in chunk_list(row_bit):
                rows = []
                for number, pair in enumerate(words):
                    group_row = group_rows[number // (n // 2)]
                    group_col = number % (n // 2)
                    rows.append(
                        e[2 * group_row + a, group_col + bp] * mask_of(pair, a, bp, lanes)
                    )
                lhs.append(jnp.concatenate(rows, 0))
                rhs.append(block(level, col_bit, a + 1 - row_bit, bp))
            out.append(dot_nt(jnp.concatenate(lhs, 1), jnp.concatenate(rhs, 1)))
        return jnp.concatenate(out, 1)

    def spread_rhs(level):
        t = transfer_ref[level]
        z = jnp.zeros_like(t)
        return [jnp.concatenate([t, z], 0), jnp.concatenate([z, t], 0)]

    for row_bit in range(2):
        u = images(3, [0], row_bit)
        b3[row_bit, 0] = (u + carried3[:, row_bit * 128 : row_bit * 128 + 128]).astype(BF)

    def descend(level, parent, child, group_rows):
        n_pairs = parent.shape[1]
        count = len(group_rows)
        value = jnp.concatenate([parent[r].reshape(n_pairs * VEC, 128) for r in group_rows], 0)
        even, odd = [
            dot_nn(value, rhs).reshape(count, n_pairs, 1, VEC, 256) for rhs in spread_rhs(level)
        ]
        carried = jnp.concatenate([even, odd], 2).reshape(count, 2 * n_pairs, VEC, 256)
        for row_bit in range(2):
            u = images(level, group_rows, row_bit).reshape(count, 2 * n_pairs, VEC, 128)
            u = u + carried[:, :, :, row_bit * 128 : row_bit * 128 + 128]
            for number, group_row in enumerate(group_rows):
                child[2 * group_row + row_bit] = u[number].astype(BF)

    descend(2, b3, b2, [0, 1])
    descend(1, b2, b1, list(range(sizes[1] // 2)))

    def loop0(k, carry):
        descend(0, b1, b0, [2 * k, 2 * k + 1])
        return carry

    lax.fori_loop(0, sizes[0] // 4, loop0, 0)

    for k in range(12, n_in - 1):
        fetch(k).wait()
    for side in range(2):
        lhs = jnp.concatenate(
            [cols[side, d : d + patch].reshape(patch * VEC, 256) for d in range(3)], 1
        )
        rhs = jnp.concatenate([tiles_ref[3 * d + 2 * side] for d in range(3)], 1)
        edge_col[side] = dot_nt(lhs, rhs).reshape(patch, VEC, 256)
    for side, ref in ((0, from_lo), (1, from_hi)):
        cells = [
            jnp.concatenate([ref[row_cells[(j, half)]] for half in range(2)], 1)
            for j in range(patch)
        ]
        zeros = jnp.zeros((VEC, 256), BF)
        lhs = jnp.concatenate(
            [
                jnp.concatenate([zeros] + cells[:-1], 0),
                jnp.concatenate(cells, 0),
                jnp.concatenate(cells[1:] + [zeros], 0),
            ],
            1,
        )
        rhs = jnp.concatenate([tiles_ref[6 * side + d] for d in range(3)], 1)
        edge_row[side] = dot_nt(lhs, rhs).reshape(patch, VEC, 256)

    basis = basis_ref[...]
    zb = jnp.zeros_like(basis)
    basis_pair = [jnp.concatenate([basis, zb], 0), jnp.concatenate([zb, basis], 0)]

    def copy(i):
        return pltpu.make_async_copy(out_buf.at[i], out_ref.at[i], sems.at[i])

    def finish(i, extra):
        fetch_acc(i).wait()
        value = b0[i].reshape(patch // 2 * VEC, 128)
        far = [dot_nn(value, rhs).reshape(patch // 2, 1, VEC, 256) for rhs in basis_pair]
        total_row = jnp.concatenate(far, 1).reshape(patch, VEC, 256) + acc_ref[i]
        if extra is not None:
            total_row = total_row + edge_row[extra]
        first = total_row[0:1] + edge_col[0, pl.ds(i, 1)]
        last = total_row[patch - 1 : patch] + edge_col[1, pl.ds(i, 1)]
        total_row = jnp.concatenate([first, total_row[1 : patch - 1], last], 0)
        out_buf[i] = total_row.astype(BF)
        copy(i).start()

    finish(0, 0)
    finish(patch - 1, 1)

    def loop_out(i, carry):
        finish(i, None)
        return carry

    lax.fori_loop(1, patch - 1, loop_out, 0)

    def loop_wait(i, carry):
        copy(i).wait()
        return carry

    lax.fori_loop(0, patch, loop_wait, 0)


def vspec():
    return pl.BlockSpec(memory_space=VMEM)


def sspec():
    return pl.BlockSpec(memory_space=pltpu.SMEM)


def shards(
    samples, leaf_basis, transfer, coupling, near_tiles,
    codes_local, counts_local, codes_upper, counts_upper,
):
    patch = samples.shape[0]
    sizes = [patch // 2**k for k in range(4)]
    n_gx = lax.axis_size("gx")
    n_gy = lax.axis_size("gy")
    units_gx = len(gx_units(sizes, patch))
    units_gy = gy_starts(sizes, patch)[2]
    params = pltpu.CompilerParams(vmem_limit_bytes=56 * 1024 * 1024)

    anywhere = pl.BlockSpec(memory_space=pl.ANY)
    shapes = [(n, n // 2, VEC, 128) for n in sizes]
    shapes += [(n_gx * n_gy, VEC // 2, 128)]
    shapes += [(units_gx, VEC, 128)] * 2 + [(units_gy + 2 * EDGE, VEC, 128)] * 2
    outs = pl.pallas_call(
        project_kernel,
        out_shape=[jax.ShapeDtypeStruct(v, BF) for v in shapes],
        in_specs=[anywhere, vspec(), vspec()],
        out_specs=[anywhere] * 9,
        scratch_shapes=[pltpu.VMEM(v, BF) for v in shapes]
        + [
            pltpu.VMEM((patch, patch, VEC, 256), BF),
            pltpu.SemaphoreType.DMA((patch,)),
            pltpu.SemaphoreType.DMA((patch,)),
            pltpu.SemaphoreType.DMA((9,)),
        ],
        compiler_params=params,
        name="project",
    )(samples, leaf_basis, transfer)
    q0, q1, q2, q3, q4, gx_lo, gx_hi, gy_left, gy_right = outs

    up = lambda n: [(i, i + 1) for i in range(n - 1)]
    dn = lambda n: [(i + 1, i) for i in range(n - 1)]
    from_lo = lax.ppermute(gx_hi, "gx", up(n_gx))
    from_hi = lax.ppermute(gx_lo, "gx", dn(n_gx))
    every = lax.all_to_all(q4, ("gx", "gy"), 0, 0, tiled=True)
    full = jax.ShapeDtypeStruct((units_gy + 2 * EDGE, VEC, 128), BF)
    send_left, send_right = pl.pallas_call(
        corner_kernel,
        out_shape=[full, full],
        in_specs=[anywhere] * 4,
        out_specs=[anywhere] * 2,
        scratch_shapes=[pltpu.VMEM((4, EDGE, VEC, 128), BF), pltpu.SemaphoreType.DMA((8,))],
        input_output_aliases={2: 0, 3: 1},
        compiler_params=params,
        name="corner",
    )(from_lo, from_hi, gy_left, gy_right)
    from_left = lax.ppermute(send_right, "gy", up(n_gy))
    from_right = lax.ppermute(send_left, "gy", dn(n_gy))

    n_words = word_offsets(sizes)[-1]
    acc, words = pl.pallas_call(
        near_kernel,
        out_shape=[
            jax.ShapeDtypeStruct((patch, patch, VEC, 256), F32),
            jax.ShapeDtypeStruct((n_words, 2, 8, 128), jnp.int32),
        ],
        in_specs=[anywhere, anywhere, vspec(), vspec()],
        out_specs=[anywhere, anywhere],
        scratch_shapes=[
            pltpu.VMEM((patch, patch, VEC, 256), BF),
            pltpu.VMEM((patch, patch, VEC, 256), F32),
            pltpu.VMEM((9 * 256, 256), BF),
            pltpu.VMEM(near_tiles.shape, BF),
            pltpu.VMEM((n_words, 2, 8, 128), jnp.int32),
            pltpu.SemaphoreType.DMA((patch,)),
            pltpu.SemaphoreType.DMA((patch // 2,)),
            pltpu.SemaphoreType.DMA((2,)),
        ],
        compiler_params=params,
        name="near",
    )(
        samples, near_tiles,
        codes_local.reshape(patch * patch, *codes_local.shape[2:]),
        counts_local.reshape(patch * patch, counts_local.shape[2]),
    )

    def padded(rows, pairs):
        return pltpu.VMEM((rows + 4, pairs + 2, VEC, 128), BF)

    inputs = [
        transfer, every, coupling, words, q0, q1, q2, q3,
        from_lo, from_hi, from_left, from_right, leaf_basis, near_tiles, acc,
    ]
    scratch = [pltpu.VMEM(v.shape, v.dtype) for v in inputs]
    scratch += [padded(n, n // 2) for n in sizes]
    scratch += [padded(n_gx // 2**k, n_gy // 2 ** (k + 1)) for k in range(3)]
    scratch += [pltpu.VMEM((5, 7, RANK, 384), BF)]
    scratch += [pltpu.VMEM((n, n // 2, VEC, 128), BF) for n in sizes]
    scratch += [
        pltpu.VMEM((2, patch + 2, VEC, 256), BF),
        pltpu.VMEM((2, patch, VEC, 256), F32),
        pltpu.VMEM((2, patch, VEC, 256), F32),
        pltpu.VMEM((patch, patch, VEC, 256), BF),
        pltpu.SemaphoreType.DMA((patch,)),
        pltpu.SemaphoreType.DMA((len(inputs) - 1,)),
        pltpu.SemaphoreType.DMA((patch,)),
    ]
    return pl.pallas_call(
        final_kernel,
        out_shape=jax.ShapeDtypeStruct((patch, patch, VEC, 256), BF),
        in_specs=[sspec(), vspec()] + [anywhere] * len(inputs),
        out_specs=pl.BlockSpec(memory_space=pl.ANY),
        scratch_shapes=scratch,
        compiler_params=params,
        name="final",
    )(
        counts_upper, codes_upper.T, *inputs,
    )


def solution(mesh):
    big = P("gx", "gy", None, None)
    in_specs = (big, P(), P(), P(), P(), big, P("gx", "gy", None), P(), P())
    return jax.shard_map(shards, mesh=mesh, in_specs=in_specs, out_specs=big, check_vma=False)
```

time: 637 us -> 81.6 us (0.13)
  the two profiles are of different devices: /device:TPU:38 before, /device:TPU:28 now
where the time goes in v1:
time: 81.6 us; the launch traced here: 81.2 us
  Pallas kernels  47.8 us (59%)
  starting transfers between devices  22.1 us (27%)
  waiting for transfers between devices  8.29 us (10%)
  local copies, waits for them, and re-layouts  2.93 us (4%)
    pallas_call x1, Pallas kernels, shards(): pl.pallas_call(final_kernel, out_shape=jax.ShapeDtypeStruct((patch, patch...  23 us
    pallas_call x1, Pallas kernels, shards(): pl.pallas_call(near_kernel, out_shape=[jax.ShapeDtypeStruct((patch, patch...  15.1 us
    all_to_all x1, starting transfers between devices, shards(): every = lax.all_to_all(q4, ('gx', 'gy'), 0, 0, tiled=True)  10.7 us
    pallas_call x1, Pallas kernels, shards(): pl.pallas_call(project_kernel, out_shape=[jax.ShapeDtypeStruct(v, BF) for...  8.06 us
    ppermute x1, waiting for transfers between devices, shards(): from_lo = lax.ppermute(gx_hi, 'gx', up(n_gx))  5.13 us
    ppermute x1, starting transfers between devices, shards(): from_hi = lax.ppermute(gx_lo, 'gx', dn(n_gx))  3.64 us
    ppermute x1, starting transfers between devices, shards(): from_left = lax.ppermute(send_right, 'gy', up(n_gy))  3.49 us
    unnamed x13, local copies, waits for them, and re-layouts  2.93 us
  transfers between devices with their start and end apart: 5, of which 3 were waited for; matrix products, arithmetic and copies ran while one was open for 1% of the time, Pallas kernels for 19%

profile of v1, /device:TPU:28, one launch (start us, length us, event | category | flops | bytes accessed | tf_op | source)
XLA Modules:
  0.0 81.2 jit_solution(480797716568743824)
XLA Ops:
  0.0 0.0 copy-start.5
  0.0 8.1 %project.1 = (bf16[16,8,32,128]{3,2,1,0:T(8,128)(2,1)}, bf16[8,4,32,128]{3,2,1,0:T(8,128)(2,1)}, bf16[4,2,32,128]{3,2,1,0:T(8,128)(2,1)}, bf16[2,1,32,128]{3,2,1...) custom-call(bf16[16,16,32,256]{3,2,1,0:T(8,128)(2,1)} %s_hbm.1, ...), custom_call_target="tpu_custom_call" | custom-call | tf_op jit(solution)/shard_map/project/pallas_call | solution.py:590
  8.1 1.9 %collective-permute-start = (bf16[64,32,128]{2,1,0:T(8,128)(2,1)}, bf16[64,32,128]{2,1,0:T(8,128)(2,1)S(1)}, u32[]{:S(2)}, u32[]{:S(2)}) collective-permute-start(bf16[64,32,128]{2,1,0:T(8,128)(2,1)} %get-tuple-element.24), channel_id=1, source_target_pairs={{0,16},{16,32},{32,48},{48,64},{64,80},{80,96},{96,112},{1,17},{17... | collective-permute-start | bytes 1572872 | tf_op jit(solution)/shard_map/ppermute | solution.py:609
  10.0 3.6 %collective-permute-start.1 = (bf16[64,32,128]{2,1,0:T(8,128)(2,1)}, bf16[64,32,128]{2,1,0:T(8,128)(2,1)S(1)}, u32[]{:S(2)}, u32[]{:S(2)}) collective-permute-start(bf16[64,32,128]{2,1,0:T(8,128)(2,1)} %get-tuple-element.25), channel_id=1, source_target_pairs={{16,0},{32,16},{48,32},{64,48},{80,64},{96,80},{112,96},{17,1},{33... | collective-permute-start | bytes 1572872 | tf_op jit(solution)/shard_map/ppermute | solution.py:610
  13.6 5.1 %collective-permute-done.from_lo.refs_8_ = bf16[64,32,128]{2,1,0:T(8,128)(2,1)S(1)} collective-permute-done((bf16[64,32,128]{2,1,0:T(8,128)(2,1)}, bf16[64,32,128]{2,1,0:T(8,128)(2,1)S(1)}, u32[]{:S(2)}, u32[]{:S(2)}) %collective-permute-start) | collective-permute-done | bytes 524320 | tf_op jit(solution)/shard_map/ppermute | solution.py:609
  18.8 1.9 %collective-permute-done.1.from_hi.refs_9_ = bf16[64,32,128]{2,1,0:T(8,128)(2,1)S(1)} collective-permute-done((bf16[64,32,128]{2,1,0:T(8,128)(2,1)}, bf16[64,32,128]{2,1,0:T(8,128)(2,1)S(1)}, u32[]{:S(2)}, u32[]{:S(2)}) %collective-permute-start.1) | collective-permute-done | bytes 524320 | tf_op jit(solution)/shard_map/ppermute | solution.py:610
  20.6 0.0 copy-start.2
  20.6 0.0 copy-done.1
  20.6 0.8 copy-done.2
  21.4 1.7 %corner.1 = (bf16[82,32,128]{2,1,0:T(8,128)(2,1)}, bf16[82,32,128]{2,1,0:T(8,128)(2,1)}) custom-call(bf16[64,32,128]{2,1,0:T(8,128)(2,1)} %copy-done.1, bf16[64,32,128]{2,1,0:T(8,128)(2,1)} %copy-done.2, bf16[82,32,128]{2,1,0:T(8,128)(2,1)} %get-tuple-element.26.left_in, ...), custom_call_target="tpu_custom_call", output_to_operand_aliasing={{0}: (2, {}), {1}: (3, {})} | custom-call | tf_op jit(solution)/shard_map/corner/pallas_call | solution.py:613
  23.2 3.5 %collective-permute-start.2 = (bf16[82,32,128]{2,1,0:T(8,128)(2,1)}, bf16[82,32,128]{2,1,0:T(8,128)(2,1)S(1)}, u32[]{:S(2)}, u32[]{:S(2)}) collective-permute-start(bf16[82,32,128]{2,1,0:T(8,128)(2,1)} %get-tuple-element.28), channel_id=1, source_target_pairs={{0,1},{1,2},{2,3},{3,4},{4,5},{5,6},{6,7},{7,8},{8,9},{9,10},{10,1... | collective-permute-start | bytes 2015240 | tf_op jit(solution)/shard_map/ppermute | solution.py:623
  26.6 2.4 %collective-permute-start.3 = (bf16[82,32,128]{2,1,0:T(8,128)(2,1)}, bf16[82,32,128]{2,1,0:T(8,128)(2,1)S(1)}, u32[]{:S(2)}, u32[]{:S(2)}) collective-permute-start(bf16[82,32,128]{2,1,0:T(8,128)(2,1)} %get-tuple-element.29), channel_id=1, source_target_pairs={{1,0},{2,1},{3,2},{4,3},{5,4},{6,5},{7,6},{8,7},{9,8},{10,9},{11,1... | collective-permute-start | bytes 2015240 | tf_op jit(solution)/shard_map/ppermute | solution.py:624
  29.0 10.7 %all-to-all-start = ((bf16[128,16,128]{2,1,0:T(8,128)(2,1)}), bf16[128,16,128]{2,1,0:T(8,128)(2,1)S(1)}, u32[]{:S(2)}, u32[]{:S(2)}) async-start(bf16[128,16,128]{2,1,0:T(8,128)(2,1)} %get-tuple-element.18), calls=%async_computation | async-start | bytes 1048576 | tf_op jit(solution)/shard_map/all_to_all | solution.py:611
  39.7 0.0 copy-done.5
  39.7 0.8 %copy.12 = s32[16,16,4]{2,1,0:T(8,128)} copy(s32[16,16,4]{1,2,0:T(4,128)S(1)} %copy-done.5) | data formatting | bytes 8192 | tf_op args[6]
  40.5 15.1 %near.1 = (f32[16,16,32,256]{3,2,1,0:T(8,128)}, s32[340,2,8,128]{3,2,1,0:T(8,128)}) custom-call(bf16[16,16,32,256]{3,2,1,0:T(8,128)(2,1)} %s_hbm.1, bf16[9,256,256]{2,1,0:T(8,128)(2,1)} %refs_13_.1, s32[256,4,27]{2,1,0:T(4,128)} %bitcast.3, s32[256,4]{1,0:T(8,128)} %bitcast.4), custom_call_target="tpu_custom_call" | custom-call | tf_op jit(solution)/shard_map/near/pallas_call | solution.py:627
  55.6 1.3 %all-to-all-done.refs_1_ = bf16[128,16,128]{2,1,0:T(8,128)(2,1)S(1)} async-done(((bf16[128,16,128]{2,1,0:T(8,128)(2,1)}), bf16[128,16,128]{2,1,0:T(8,128)(2,1)S(1)}, u32[]{:S(2)}, u32[]{:S(2)}) %all-to-all-start) | async-done | bytes 524320 | tf_op jit(solution)/shard_map/all_to_all | solution.py:611
  56.9 0.0 collective-permute-done.2.refs_10_
  56.9 0.0 collective-permute-done.3.refs_11_
  56.9 0.0 copy-start.4
  56.9 0.8 copy-done
  57.7 0.2 copy-done.3
  57.9 0.3 copy-done.4
  58.2 23.0 %final.1 = bf16[16,16,32,256]{3,2,1,0:T(8,128)(2,1)} custom-call(s32[168]{0:T(256)} %counts_upper_ref.1, s32[27,168]{1,0:T(8,128)} %bitcast.5, bf16[5,64,256]{2,1,0:T(8,128)(2,1)} %refs_0_.1, bf16[128,16,128]{2,1,0:T(8,128)(2,1)} %copy-done, bf16[5,7,64,448]{3,2,1,0:T(8,128)(2,1)} %refs_2_.1, s32[340,2,8,128]{3,2,1,0:T(8,128)} %get-tuple-element.19.refs_3_, ...), custom_call_target="tpu_custom_call" | custom-call | tf_op jit(solution)/shard_map/final/pallas_call | solution.py:674
  (3 shorter events, 0.0 us)
Async XLA Ops:
  0.0 39.7 %copy-start.5 = (s32[16,16,4]{1,2,0:T(4,128)S(1)}, s32[16,16,4]{1,2,0:T(4,128)}, u32[]{:S(2)}) copy-start(s32[16,16,4]{1,2,0:T(4,128)} %param.15) | copy-start | bytes 12292
  8.1 10.7 %collective-permute-start = (bf16[64,32,128]{2,1,0:T(8,128)(2,1)}, bf16[64,32,128]{2,1,0:T(8,128)(2,1)S(1)}, u32[]{:S(2)}, u32[]{:S(2)}) collective-permute-start(bf16[64,32,128]{2,1,0:T(8,128)(2,1)} %get-tuple-element.24), channel_id=1, source_target_pairs={{0,16},{16,32},{32,48},{48,64},{64,80},{80,96},{96,112},{1,17},{17... | collective-permute-start | bytes 1572872 | tf_op jit(solution)/shard_map/ppermute | solution.py:609
  10.0 10.6 %collective-permute-start.1 = (bf16[64,32,128]{2,1,0:T(8,128)(2,1)}, bf16[64,32,128]{2,1,0:T(8,128)(2,1)S(1)}, u32[]{:S(2)}, u32[]{:S(2)}) collective-permute-start(bf16[64,32,128]{2,1,0:T(8,128)(2,1)} %get-tuple-element.25), channel_id=1, source_target_pairs={{16,0},{32,16},{48,32},{64,48},{80,64},{96,80},{112,96},{17,1},{33... | collective-permute-start | bytes 1572872 | tf_op jit(solution)/shard_map/ppermute | solution.py:610
  18.8 1.9 %copy-start.1 = (bf16[64,32,128]{2,1,0:T(8,128)(2,1)}, bf16[64,32,128]{2,1,0:T(8,128)(2,1)S(1)}, u32[]{:S(2)}) copy-start(bf16[64,32,128]{2,1,0:T(8,128)(2,1)S(1)} %collective-permute-done.from_lo.refs_8_) | copy-start | bytes 1572868
  20.6 0.8 copy-start.2
  23.2 33.7 %collective-permute-start.2 = (bf16[82,32,128]{2,1,0:T(8,128)(2,1)}, bf16[82,32,128]{2,1,0:T(8,128)(2,1)S(1)}, u32[]{:S(2)}, u32[]{:S(2)}) collective-permute-start(bf16[82,32,128]{2,1,0:T(8,128)(2,1)} %get-tuple-element.28), channel_id=1, source_target_pairs={{0,1},{1,2},{2,3},{3,4},{4,5},{5,6},{6,7},{7,8},{8,9},{9,10},{10,1... | collective-permute-start | bytes 2015240 | tf_op jit(solution)/shard_map/ppermute | solution.py:623
  26.6 30.2 %collective-permute-start.3 = (bf16[82,32,128]{2,1,0:T(8,128)(2,1)}, bf16[82,32,128]{2,1,0:T(8,128)(2,1)S(1)}, u32[]{:S(2)}, u32[]{:S(2)}) collective-permute-start(bf16[82,32,128]{2,1,0:T(8,128)(2,1)} %get-tuple-element.29), channel_id=1, source_target_pairs={{1,0},{2,1},{3,2},{4,3},{5,4},{6,5},{7,6},{8,7},{9,8},{10,9},{11,1... | collective-permute-start | bytes 2015240 | tf_op jit(solution)/shard_map/ppermute | solution.py:624
  29.0 27.8 %all-to-all-start = ((bf16[128,16,128]{2,1,0:T(8,128)(2,1)}), bf16[128,16,128]{2,1,0:T(8,128)(2,1)S(1)}, u32[]{:S(2)}, u32[]{:S(2)}) async-start(bf16[128,16,128]{2,1,0:T(8,128)(2,1)} %get-tuple-element.18), calls=%async_computation | async-start | bytes 1048576 | tf_op jit(solution)/shard_map/all_to_all | solution.py:611
  56.9 0.8 copy-start
  56.9 1.0 %copy-start.3 = (bf16[82,32,128]{2,1,0:T(8,128)(2,1)}, bf16[82,32,128]{2,1,0:T(8,128)(2,1)S(1)}, u32[]{:S(2)}) copy-start(bf16[82,32,128]{2,1,0:T(8,128)(2,1)S(1)} %collective-permute-done.2.refs_10_) | copy-start | bytes 2015236
  56.9 1.3 %copy-start.4 = (bf16[82,32,128]{2,1,0:T(8,128)(2,1)}, bf16[82,32,128]{2,1,0:T(8,128)(2,1)S(1)}, u32[]{:S(2)}) copy-start(bf16[82,32,128]{2,1,0:T(8,128)(2,1)S(1)} %collective-permute-done.3.refs_11_) | copy-start | bytes 2015236

commit v2 on v1

--- a/solution.py
+++ b/solution.py
@@ -76,8 +76,9 @@
     return starts, at, at + 2 * patch
 
 
-def project_kernel(hbm_ref, basis_ref, transfer_ref, *refs):
-    outs, bufs, (s_ref, sems, row_sems, out_sems) = refs[:9], refs[9:18], refs[18:]
+def project_kernel(hbm_ref, basis_hbm, transfer_hbm, *refs):
+    outs, bufs = refs[:9], refs[9:18]
+    s_ref, basis_ref, transfer_ref, sems, row_sems, out_sems, more_sems = refs[18:]
     q0, q1, q2, q3, q4, gx_lo, gx_hi, gy_left, gy_right = bufs
     patch = s_ref.shape[0]
     qs = [q0, q1, q2, q3]
@@ -96,7 +97,12 @@
         copy(i).start()
         return carry
 
+    get_basis = pltpu.make_async_copy(basis_hbm, basis_ref, more_sems.at[0])
+    get_transfer = pltpu.make_async_copy(transfer_hbm, transfer_ref, more_sems.at[1])
+    get_basis.start()
     lax.fori_loop(0, patch, fetch, 0)
+    get_transfer.start()
+    get_basis.wait()
     basis = pair_rhs(basis_ref[...])
     starts, base, _ = gy_starts(sizes, patch)
 
@@ -111,6 +117,7 @@
         return carry
 
     lax.fori_loop(0, patch, row, 0)
+    get_transfer.wait()
     for level in range(3):
         rhs = pair_rhs(transfer_ref[level])
         for r in range(sizes[level + 1]):
@@ -186,6 +193,10 @@
     return words
 
 
+def half_sizes(patch):
+    return [patch // 2**k for k in range(4)]
+
+
 def word_offsets(sizes):
     offsets = [0]
     for n in sizes:
@@ -194,8 +205,9 @@
 
 
 def near_kernel(
-    s_hbm, tiles_hbm, codes_ref, counts_ref, acc_hbm, words_hbm,
-    s_ref, acc_ref, w_ref, tiles_ref, words_ref, in_sems, out_sems, more_sems,
+    s_hbm, tiles_hbm, codes_hbm, counts_hbm, lo_hbm, hi_hbm, acc_hbm, words_hbm,
+    s_ref, acc_ref, w_ref, tiles_ref, words_ref, codes_ref, counts_ref, lo_ref, hi_ref,
+    in_sems, out_sems, more_sems,
 ):
     patch = s_ref.shape[0]
 
@@ -210,10 +222,16 @@
         fetch(i).start()
         return carry
 
+    pairs = [(codes_hbm, codes_ref), (counts_hbm, counts_ref), (lo_hbm, lo_ref), (hi_hbm, hi_ref)]
+    more = [pltpu.make_async_copy(a, b, more_sems.at[2 + k]) for k, (a, b) in enumerate(pairs)]
+    for copy in more:
+        copy.start()
     fetch_tiles = pltpu.make_async_copy(tiles_hbm, tiles_ref, more_sems.at[0])
     put_words = pltpu.make_async_copy(words_ref, words_hbm, more_sems.at[1])
     fetch_tiles.start()
     lax.fori_loop(0, patch, start_fetch, 0)
+    for copy in more:
+        copy.wait()
     levels = counts_ref.shape[1]
     at = 0
     for level in range(levels):
@@ -223,10 +241,14 @@
         for group, power in enumerate(list_words(codes, counts)):
             word = jnp.sum(power, axis=1, keepdims=True).astype(jnp.int32)
             word = jnp.broadcast_to(word, (patch * patch, 128))
+            if level == 0:
+                words_ref[group, 0 : n * n] = word
+                continue
             for i in range(n):
                 for j in range(n):
-                    r = ((i * patch + j) << level)
-                    words_ref[at + i * n + j, group] = jnp.broadcast_to(word[r : r + 1], (8, 128))
+                    r = (i * patch + j) << level
+                    k = at + i * n + j
+                    words_ref[group, k : k + 1] = word[r : r + 1]
         at += n * n
     put_words.start()
     fetch_tiles.wait()
@@ -243,8 +265,7 @@
 
     def put(i, rows):
         blocks = [
-            jnp.zeros((patch * VEC, 256), BF) if r is None else s_ref[r].reshape(patch * VEC, 256)
-            for r in rows
+            r if getattr(r, "ndim", 0) == 2 else s_ref[r].reshape(patch * VEC, 256) for r in rows
         ]
         lhs = []
         for d in range(3):
@@ -255,7 +276,18 @@
 
     for i in range(3):
         fetch(i).wait()
-    put(0, [None, 0, 1, 2])
+    cells = {unit[1:]: k for k, unit in enumerate(gx_units(half_sizes(patch), patch)) if unit[0] == "s"}
+
+    def halo_row(ref):
+        return jnp.concatenate(
+            [
+                jnp.concatenate([ref[cells[(j, half)]] for j in range(patch)], 0)
+                for half in range(2)
+            ],
+            1,
+        )
+
+    put(0, [halo_row(lo_ref), 0, 1, 2])
     put_out(0).start()
 
     def row(k, carry):
@@ -268,7 +300,7 @@
 
     lax.fori_loop(1, patch // 2 - 1, row, 0)
     fetch(patch - 1).wait()
-    put(patch - 2, [patch - 3, patch - 2, patch - 1, None])
+    put(patch - 2, [patch - 3, patch - 2, patch - 1, halo_row(hi_ref)])
     put_out(patch // 2 - 1).start()
 
     def wait_out(k, carry):
@@ -301,51 +333,20 @@
     return jnp.concatenate([m, m, m, m], 0).astype(BF)
 
 
-def final_kernel(
-    counts_upper_ref, codes_upper_ref,
-    *refs,
+def upper_kernel(
+    counts_upper_ref, codes_upper_ref, every_hbm, transfer_hbm, coupling_hbm, out_ref,
+    every, transfer_ref, coupling_ref, shifted, f4, f5, f6, sems,
 ):
-    n_in = 15
-    sources, out_ref, buffers, rest = refs[:n_in], refs[n_in], refs[n_in + 1 : 2 * n_in + 1], refs[2 * n_in + 1 :]
-    (
-        transfer_ref, every, coupling_ref, words_ref, q0, q1, q2, q3,
-        from_lo, from_hi, from_left, from_right, basis_ref, tiles_ref, acc_ref,
-    ) = buffers
-    (
-    e0, e1, e2, e3, f4, f5, f6, shifted, b0, b1, b2, b3, cols, edge_col, edge_row, out_buf, sems, in_sems, acc_sems,
-    ) = rest
-    patch = acc_ref.shape[0]
-
-    def fetch(k):
-        return pltpu.make_async_copy(sources[k], buffers[k], in_sems.at[k])
-
-    def fetch_acc(i):
-        return pltpu.make_async_copy(sources[n_in - 1].at[i], acc_ref.at[i], acc_sems.at[i])
-
-    for k in range(n_in - 1):
-        fetch(k).start()
-
-    def start_acc(i, carry):
-        fetch_acc(i).start()
-        return carry
-
-    lax.fori_loop(0, patch, start_acc, 0)
-    qs = [q0, q1, q2, q3]
-    es = [e0, e1, e2, e3]
-    sizes = [q.shape[0] for q in qs]
+    pairs = [(every_hbm, every), (transfer_hbm, transfer_ref)]
+    pairs += [(coupling_hbm.at[coupling_hbm.shape[0] - 1], coupling_ref)]
+    copies = [pltpu.make_async_copy(a, b, sems.at[k]) for k, (a, b) in enumerate(pairs)]
+    for copy in copies:
+        copy.start()
     lanes = lane_bits()
-    word_at = word_offsets(sizes)
-
-    for k in range(3):
-        fetch(k).wait()
-    for level in range(5):
-        for d in range(7):
-            shifted[level, d] = coupling_ref[level, d, :, 64:448]
-
-    def block(level, col_bit, d, bp):
-        if col_bit == 1:
-            return coupling_ref[level, d, :, bp * 128 : bp * 128 + 128]
-        return shifted[level, d, :, bp * 128 : bp * 128 + 128]
+    for copy in copies:
+        copy.wait()
+    for d in range(7):
+        shifted[d] = coupling_ref[d, :, 64:448]
 
     f4[...] = jnp.zeros_like(f4)
     f5[...] = jnp.zeros_like(f5)
@@ -403,8 +404,8 @@
         for a in range(6):
             for bp in range(3):
                 lhs.append(f[top_row + a, left + bp] * mask_of(words, a, bp, lanes))
-            even = shifted[4, a + 1 - rb]
-            odd = coupling_ref[4, a + 1 - rb][:, 0:384]
+            even = shifted[a + 1 - rb]
+            odd = coupling_ref[a + 1 - rb][:, 0:384]
             rhs.append(jnp.where(cb == 1, odd, even))
         uppers.append(dot_nt(jnp.concatenate(lhs, 1), jnp.concatenate(rhs, 1)))
     down = uppers[-1]
@@ -415,21 +416,73 @@
         half = jnp.where((r_here & 1) == 1, carried[:, 128:256], carried[:, 0:128])
         half = jnp.where((c_here & 1) == 1, pltpu.roll(half, 64, 1), half)
         down = uppers[step] + half[:, 0:64]
-    carried3 = dot_nn(down.astype(BF), transfer_ref[3])
-
-    for k in range(3, 12):
+    out_ref[...] = dot_nn(down.astype(BF), transfer_ref[3])
+
+
+def final_kernel(
+    *refs,
+):
+    n_in = 14
+    sources, coupling_hbm, out_ref = refs[:n_in], refs[n_in], refs[n_in + 1]
+    buffers, rest = refs[n_in + 2 : 2 * n_in + 2], refs[2 * n_in + 2 :]
+    (
+        transfer_ref, carried_ref, words_ref, q0, q1, q2, q3,
+        from_lo, from_hi, from_left, from_right, basis_ref, tiles_ref, acc_ref,
+    ) = buffers
+    (
+    e0, e1, e2, e3, shifted, b0, b1, b2, b3, cols, edge_col, out_buf, coupling_ref,
+    sems, in_sems, acc_sems, level_sems,
+    ) = rest
+    patch = acc_ref.shape[0]
+
+    def fetch(k):
+        return pltpu.make_async_copy(sources[k], buffers[k], in_sems.at[k])
+
+    def fetch_acc(i):
+        return pltpu.make_async_copy(sources[n_in - 1].at[i], acc_ref.at[i], acc_sems.at[i])
+
+    def fetch_level(level):
+        return pltpu.make_async_copy(
+            coupling_hbm.at[level], coupling_ref.at[level], level_sems.at[level]
+        )
+
+    for k in range(11):
+        fetch(k).start()
+    for level in (3, 2, 1, 0):
+        fetch_level(level).start()
+    for k in range(11, n_in - 1):
+        fetch(k).start()
+
+    def start_acc(i, carry):
+        fetch_acc(i).start()
+        return carry
+
+    qs = [q0, q1, q2, q3]
+    es = [e0, e1, e2, e3]
+    sizes = [q.shape[0] for q in qs]
+    lanes = lane_bits()
+    word_at = word_offsets(sizes)
+
+    def get_level(level):
+        fetch_level(level).wait()
+        for d in range(7):
+            shifted[level, d] = coupling_ref[level, d, :, 64:448]
+
+    def block(level, col_bit, d, bp):
+        if col_bit == 1:
+            return coupling_ref[level, d, :, bp * 128 : bp * 128 + 128]
+        return shifted[level, d, :, bp * 128 : bp * 128 + 128]
+
+    for k in range(11):
         fetch(k).wait()
     for level in range(4):
         n = sizes[level]
         es[level][2 : n + 2, 1 : n // 2 + 1] = qs[level][...]
-    row_cells = {}
     for number, unit in enumerate(gx_units(sizes, patch)):
         if unit[0] == "q":
             _, level, r, p = unit
             es[level][r, p + 1] = from_lo[number]
             es[level][sizes[level] + 2 + r, p + 1] = from_hi[number]
-        else:
-            row_cells[unit[1:]] = number
     starts, base, total = gy_starts(sizes, patch)
     for side, ref in ((0, from_left), (1, from_right)):
         for level in range(4):
@@ -456,7 +509,12 @@
             for group_row in group_rows:
                 for group_col in range(n // 2):
                     at = word_at[level] + (2 * group_row + row_bit) * n + 2 * group_col + col_bit
-                    words.append((words_ref[at, 0], words_ref[at, 1]))
+                    words.append(
+                        [
+                            jnp.broadcast_to(words_ref[g, pl.ds(at, 1)], (8, 128))
+                            for g in range(2)
+                        ]
+                    )
             for a, bp in chunk_list(row_bit):
                 rows = []
                 for number, pair in enumerate(words):
@@ -475,6 +533,10 @@
         z = jnp.zeros_like(t)
         return [jnp.concatenate([t, z], 0), jnp.concatenate([z, t], 0)]
 
+    lax.fori_loop(0, patch, start_acc, 0)
+    for level in (3, 2, 1, 0):
+        get_level(level)
+    carried3 = carried_ref[...]
     for row_bit in range(2):
         u = images(3, [0], row_bit)
         b3[row_bit, 0] = (u + carried3[:, row_bit * 128 : row_bit * 128 + 128]).astype(BF)
@@ -502,7 +564,7 @@
 
     lax.fori_loop(0, sizes[0] // 4, loop0, 0)
 
-    for k in range(12, n_in - 1):
+    for k in range(11, n_in - 1):
         fetch(k).wait()
     for side in range(2):
         lhs = jnp.concatenate(
@@ -510,23 +572,6 @@
         )
         rhs = jnp.concatenate([tiles_ref[3 * d + 2 * side] for d in range(3)], 1)
         edge_col[side] = dot_nt(lhs, rhs).reshape(patch, VEC, 256)
-    for side, ref in ((0, from_lo), (1, from_hi)):
-        cells = [
-            jnp.concatenate([ref[row_cells[(j, half)]] for half in range(2)], 1)
-            for j in range(patch)
-        ]
-        zeros = jnp.zeros((VEC, 256), BF)
-        lhs = jnp.concatenate(
-            [
-                jnp.concatenate([zeros] + cells[:-1], 0),
-                jnp.concatenate(cells, 0),
-                jnp.concatenate(cells[1:] + [zeros], 0),
-            ],
-            1,
-        )
-        rhs = jnp.concatenate([tiles_ref[6 * side + d] for d in range(3)], 1)
-        edge_row[side] = dot_nt(lhs, rhs).reshape(patch, VEC, 256)
-
     basis = basis_ref[...]
     zb = jnp.zeros_like(basis)
     basis_pair = [jnp.concatenate([basis, zb], 0), jnp.concatenate([zb, basis], 0)]
@@ -534,27 +579,19 @@
     def copy(i):
         return pltpu.make_async_copy(out_buf.at[i], out_ref.at[i], sems.at[i])
 
-    def finish(i, extra):
+    def finish(i, carry):
         fetch_acc(i).wait()
         value = b0[i].reshape(patch // 2 * VEC, 128)
         far = [dot_nn(value, rhs).reshape(patch // 2, 1, VEC, 256) for rhs in basis_pair]
         total_row = jnp.concatenate(far, 1).reshape(patch, VEC, 256) + acc_ref[i]
-        if extra is not None:
-            total_row = total_row + edge_row[extra]
         first = total_row[0:1] + edge_col[0, pl.ds(i, 1)]
         last = total_row[patch - 1 : patch] + edge_col[1, pl.ds(i, 1)]
         total_row = jnp.concatenate([first, total_row[1 : patch - 1], last], 0)
         out_buf[i] = total_row.astype(BF)
         copy(i).start()
-
-    finish(0, 0)
-    finish(patch - 1, 1)
-
-    def loop_out(i, carry):
-        finish(i, None)
-        return carry
-
-    lax.fori_loop(1, patch - 1, loop_out, 0)
+        return carry
+
+    lax.fori_loop(0, patch, finish, 0)
 
     def loop_wait(i, carry):
         copy(i).wait()
@@ -590,14 +627,17 @@
     outs = pl.pallas_call(
         project_kernel,
         out_shape=[jax.ShapeDtypeStruct(v, BF) for v in shapes],
-        in_specs=[anywhere, vspec(), vspec()],
+        in_specs=[anywhere] * 3,
         out_specs=[anywhere] * 9,
         scratch_shapes=[pltpu.VMEM(v, BF) for v in shapes]
         + [
             pltpu.VMEM((patch, patch, VEC, 256), BF),
+            pltpu.VMEM(leaf_basis.shape, BF),
+            pltpu.VMEM(transfer.shape, BF),
             pltpu.SemaphoreType.DMA((patch,)),
             pltpu.SemaphoreType.DMA((patch,)),
             pltpu.SemaphoreType.DMA((9,)),
+            pltpu.SemaphoreType.DMA((2,)),
         ],
         compiler_params=params,
         name="project",
@@ -623,64 +663,84 @@
     from_left = lax.ppermute(send_right, "gy", up(n_gy))
     from_right = lax.ppermute(send_left, "gy", dn(n_gy))
 
-    n_words = word_offsets(sizes)[-1]
+    n_words = -(-word_offsets(sizes)[-1] // 8) * 8
+    codes = codes_local.reshape(patch * patch, *codes_local.shape[2:])
+    counts = counts_local.reshape(patch * patch, counts_local.shape[2])
     acc, words = pl.pallas_call(
         near_kernel,
         out_shape=[
             jax.ShapeDtypeStruct((patch, patch, VEC, 256), F32),
-            jax.ShapeDtypeStruct((n_words, 2, 8, 128), jnp.int32),
+            jax.ShapeDtypeStruct((2, n_words, 128), jnp.int32),
         ],
-        in_specs=[anywhere, anywhere, vspec(), vspec()],
+        in_specs=[anywhere] * 6,
         out_specs=[anywhere, anywhere],
         scratch_shapes=[
             pltpu.VMEM((patch, patch, VEC, 256), BF),
             pltpu.VMEM((patch, patch, VEC, 256), F32),
             pltpu.VMEM((9 * 256, 256), BF),
             pltpu.VMEM(near_tiles.shape, BF),
-            pltpu.VMEM((n_words, 2, 8, 128), jnp.int32),
+            pltpu.VMEM((2, n_words, 128), jnp.int32),
+            pltpu.VMEM(codes.shape, codes.dtype),
+            pltpu.VMEM(counts.shape, counts.dtype),
+            pltpu.VMEM(from_lo.shape, BF),
+            pltpu.VMEM(from_hi.shape, BF),
             pltpu.SemaphoreType.DMA((patch,)),
             pltpu.SemaphoreType.DMA((patch // 2,)),
-            pltpu.SemaphoreType.DMA((2,)),
+            pltpu.SemaphoreType.DMA((6,)),
         ],
         compiler_params=params,
         name="near",
     )(
-        samples, near_tiles,
-        codes_local.reshape(patch * patch, *codes_local.shape[2:]),
-        counts_local.reshape(patch * patch, counts_local.shape[2]),
+        samples, near_tiles, codes, counts, from_lo, from_hi,
     )
 
     def padded(rows, pairs):
         return pltpu.VMEM((rows + 4, pairs + 2, VEC, 128), BF)
 
+    carried = pl.pallas_call(
+        upper_kernel,
+        out_shape=jax.ShapeDtypeStruct((VEC, transfer.shape[2]), F32),
+        in_specs=[sspec(), vspec()] + [anywhere] * 3,
+        out_specs=vspec(),
+        scratch_shapes=[
+            pltpu.VMEM(every.shape, BF),
+            pltpu.VMEM(transfer.shape, BF),
+            pltpu.VMEM(coupling.shape[1:], BF),
+            pltpu.VMEM((7, RANK, 384), BF),
+        ]
+        + [padded(n_gx // 2**k, n_gy // 2 ** (k + 1)) for k in range(3)]
+        + [pltpu.SemaphoreType.DMA((3,))],
+        compiler_params=params,
+        name="upper",
+    )(counts_upper, codes_upper.T, every, transfer, coupling)
     inputs = [
-        transfer, every, coupling, words, q0, q1, q2, q3,
+        transfer, carried, words, q0, q1, q2, q3,
         from_lo, from_hi, from_left, from_right, leaf_basis, near_tiles, acc,
     ]
     scratch = [pltpu.VMEM(v.shape, v.dtype) for v in inputs]
     scratch += [padded(n, n // 2) for n in sizes]
-    scratch += [padded(n_gx // 2**k, n_gy // 2 ** (k + 1)) for k in range(3)]
-    scratch += [pltpu.VMEM((5, 7, RANK, 384), BF)]
+    scratch += [pltpu.VMEM((4, 7, RANK, 384), BF)]
     scratch += [pltpu.VMEM((n, n // 2, VEC, 128), BF) for n in sizes]
     scratch += [
         pltpu.VMEM((2, patch + 2, VEC, 256), BF),
         pltpu.VMEM((2, patch, VEC, 256), F32),
-        pltpu.VMEM((2, patch, VEC, 256), F32),
         pltpu.VMEM((patch, patch, VEC, 256), BF),
+        pltpu.VMEM((4, *coupling.shape[1:]), BF),
         pltpu.SemaphoreType.DMA((patch,)),
         pltpu.SemaphoreType.DMA((len(inputs) - 1,)),
         pltpu.SemaphoreType.DMA((patch,)),
+        pltpu.SemaphoreType.DMA((4,)),
     ]
     return pl.pallas_call(
         final_kernel,
         out_shape=jax.ShapeDtypeStruct((patch, patch, VEC, 256), BF),
-        in_specs=[sspec(), vspec()] + [anywhere] * len(inputs),
+        in_specs=[anywhere] * (len(inputs) + 1),
         out_specs=pl.BlockSpec(memory_space=pl.ANY),
         scratch_shapes=scratch,
         compiler_params=params,
         name="final",
     )(
-        counts_upper, codes_upper.T, *inputs,
+        *inputs, coupling,
     )
 
 

time: 81.6 us -> 99.2 us (1.22)
  waiting for transfers between devices: 8.29 us -> 23.3 us
  Pallas kernels: 47.8 us -> 49.8 us
    all_to_all x1, waiting for transfers between devices: 1.29 us -> 16.3 us  [shards(): every = lax.all_to_all(q4, ('gx', 'gy'), 0, 0, tiled=True)]
    pallas_call x0 -> x1, Pallas kernels: none -> 4.29 us  [shards(): pl.pallas_call(upper_kernel, out_shape=jax.ShapeDtypeStruct((VEC, transfe...]
    pallas_call x1, Pallas kernels: 23 us -> 21.4 us  [shards(): pl.pallas_call(final_kernel, out_shape=jax.ShapeDtypeStruct((patch, patch...]
  transfers between devices with their start and end apart: 5 -> 5, of which waited for: 3 -> 3; matrix products, arithmetic and copies ran while one was open for 1% -> 1% of each run, Pallas kernels for 19% -> 20%
where the time goes in v2:
time: 99.2 us; the launch traced here: 98.8 us
  Pallas kernels  49.8 us (50%)
  waiting for transfers between devices  23.3 us (23%)
  starting transfers between devices  22.1 us (22%)
  local copies, waits for them, and re-layouts  3.53 us (4%)
    pallas_call x1, Pallas kernels, shards(): pl.pallas_call(final_kernel, out_shape=jax.ShapeDtypeStruct((patch, patch...  21.4 us
    all_to_all x1, waiting for transfers between devices, shards(): every = lax.all_to_all(q4, ('gx', 'gy'), 0, 0, tiled=True)  16.3 us
    pallas_call x1, Pallas kernels, shards(): pl.pallas_call(near_kernel, out_shape=[jax.ShapeDtypeStruct((patch, patch...  15.3 us
    all_to_all x1, starting transfers between devices, shards(): every = lax.all_to_all(q4, ('gx', 'gy'), 0, 0, tiled=True)  10.7 us
    pallas_call x1, Pallas kernels, shards(): pl.pallas_call(project_kernel, out_shape=[jax.ShapeDtypeStruct(v, BF) for...  7.13 us
    ppermute x1, waiting for transfers between devices, shards(): from_lo = lax.ppermute(gx_hi, 'gx', up(n_gx))  5.13 us
    pallas_call x1, Pallas kernels, shards(): pl.pallas_call(upper_kernel, out_shape=jax.ShapeDtypeStruct((VEC, transfe...  4.29 us
    ppermute x1, starting transfers between devices, shards(): from_hi = lax.ppermute(gx_lo, 'gx', dn(n_gx))  3.64 us
  transfers between devices with their start and end apart: 5, of which 3 were waited for; matrix products, arithmetic and copies ran while one was open for 1% of the time, Pallas kernels for 20%

profile of v2, /device:TPU:28, one launch (start us, length us, event | category | flops | bytes accessed | tf_op | source)
XLA Modules:
  0.0 98.8 jit_solution(11206036965639506595)
XLA Ops:
  0.0 7.1 %project.1 = (bf16[16,8,32,128]{3,2,1,0:T(8,128)(2,1)}, bf16[8,4,32,128]{3,2,1,0:T(8,128)(2,1)}, bf16[4,2,32,128]{3,2,1,0:T(8,128)(2,1)}, bf16[2,1,32,128]{3,2,1...) custom-call(bf16[16,16,32,256]{3,2,1,0:T(8,128)(2,1)} %s_hbm.1, ...), custom_call_target="tpu_custom_call" | custom-call | tf_op jit(solution)/shard_map/project/pallas_call | solution.py:627
  7.1 1.9 %collective-permute-start = (bf16[64,32,128]{2,1,0:T(8,128)(2,1)}, bf16[64,32,128]{2,1,0:T(8,128)(2,1)S(1)}, u32[]{:S(2)}, u32[]{:S(2)}) collective-permute-start(bf16[64,32,128]{2,1,0:T(8,128)(2,1)} %get-tuple-element.19), channel_id=1, source_target_pairs={{0,16},{16,32},{32,48},{48,64},{64,80},{80,96},{96,112},{1,17},{17... | collective-permute-start | bytes 1572872 | tf_op jit(solution)/shard_map/ppermute | solution.py:649
  9.1 3.6 %collective-permute-start.1 = (bf16[64,32,128]{2,1,0:T(8,128)(2,1)}, bf16[64,32,128]{2,1,0:T(8,128)(2,1)S(1)}, u32[]{:S(2)}, u32[]{:S(2)}) collective-permute-start(bf16[64,32,128]{2,1,0:T(8,128)(2,1)} %get-tuple-element.20), channel_id=1, source_target_pairs={{16,0},{32,16},{48,32},{64,48},{80,64},{96,80},{112,96},{17,1},{33... | collective-permute-start | bytes 1572872 | tf_op jit(solution)/shard_map/ppermute | solution.py:650
  12.7 5.1 %collective-permute-done.lo_hbm.from_lo.refs_7_ = bf16[64,32,128]{2,1,0:T(8,128)(2,1)S(1)} collective-permute-done((bf16[64,32,128]{2,1,0:T(8,128)(2,1)}, bf16[64,32,128]{2,1,0:T(8,128)(2,1)S(1)}, u32[]{:S(2)}, u32[]{:S(2)}) %collective-permute-start) | collective-permute-done | bytes 524320 | tf_op jit(solution)/shard_map/ppermute | solution.py:649
  17.9 1.9 %collective-permute-done.1.hi_hbm.from_hi.refs_8_ = bf16[64,32,128]{2,1,0:T(8,128)(2,1)S(1)} collective-permute-done((bf16[64,32,128]{2,1,0:T(8,128)(2,1)}, bf16[64,32,128]{2,1,0:T(8,128)(2,1)S(1)}, u32[]{:S(2)}, u32[]{:S(2)}) %collective-permute-start.1) | collective-permute-done | bytes 524320 | tf_op jit(solution)/shard_map/ppermute | solution.py:650
  19.7 0.0 copy-done
  19.7 0.8 copy-done.1
  20.5 1.7 %corner.1 = (bf16[82,32,128]{2,1,0:T(8,128)(2,1)}, bf16[82,32,128]{2,1,0:T(8,128)(2,1)}) custom-call(bf16[64,32,128]{2,1,0:T(8,128)(2,1)} %copy-done, bf16[64,32,128]{2,1,0:T(8,128)(2,1)} %copy-done.1, bf16[82,32,128]{2,1,0:T(8,128)(2,1)} %get-tuple-element.26.left_in, ...), custom_call_target="tpu_custom_call", output_to_operand_aliasing={{0}: (2, {}), {1}: (3, {})} | custom-call | tf_op jit(solution)/shard_map/corner/pallas_call | solution.py:653
  22.2 3.5 %collective-permute-start.2 = (bf16[82,32,128]{2,1,0:T(8,128)(2,1)}, bf16[82,32,128]{2,1,0:T(8,128)(2,1)S(1)}, u32[]{:S(2)}, u32[]{:S(2)}) collective-permute-start(bf16[82,32,128]{2,1,0:T(8,128)(2,1)} %get-tuple-element.28), channel_id=1, source_target_pairs={{0,1},{1,2},{2,3},{3,4},{4,5},{5,6},{6,7},{7,8},{8,9},{9,10},{10,1... | collective-permute-start | bytes 2015240 | tf_op jit(solution)/shard_map/ppermute | solution.py:663
  25.7 2.4 %collective-permute-start.3 = (bf16[82,32,128]{2,1,0:T(8,128)(2,1)}, bf16[82,32,128]{2,1,0:T(8,128)(2,1)S(1)}, u32[]{:S(2)}, u32[]{:S(2)}) collective-permute-start(bf16[82,32,128]{2,1,0:T(8,128)(2,1)} %get-tuple-element.29), channel_id=1, source_target_pairs={{1,0},{2,1},{3,2},{4,3},{5,4},{6,5},{7,6},{8,7},{9,8},{10,9},{11,1... | collective-permute-start | bytes 2015240 | tf_op jit(solution)/shard_map/ppermute | solution.py:664
  28.1 10.7 %all-to-all-start = ((bf16[128,16,128]{2,1,0:T(8,128)(2,1)}), bf16[128,16,128]{2,1,0:T(8,128)(2,1)S(1)}, u32[]{:S(2)}, u32[]{:S(2)}) async-start(bf16[128,16,128]{2,1,0:T(8,128)(2,1)} %get-tuple-element.18), calls=%async_computation | async-start | bytes 1048576 | tf_op jit(solution)/shard_map/all_to_all | solution.py:651
  38.7 0.0 copy-done.5
  38.8 0.8 copy.12
  39.6 16.3 %all-to-all-done.every_hbm = bf16[128,16,128]{2,1,0:T(8,128)(2,1)S(1)} async-done(((bf16[128,16,128]{2,1,0:T(8,128)(2,1)}), bf16[128,16,128]{2,1,0:T(8,128)(2,1)S(1)}, u32[]{:S(2)}, u32[]{:S(2)}) %all-to-all-start) | async-done | bytes 524320 | tf_op jit(solution)/shard_map/all_to_all | solution.py:651
  55.9 0.8 copy-done.2
  56.7 4.3 %upper.1.refs_1_ = f32[32,256]{1,0:T(8,128)} custom-call(s32[168]{0:T(256)} %counts_upper_ref.1, s32[27,168]{1,0:T(8,128)} %bitcast.5, bf16[128,16,128]{2,1,0:T(8,128)(2,1)} %copy-done.2, bf16[5,64,256]{2,1,0:T(8,128)(2,1)} %refs_0_.1, bf16[5,7,64,448]{3,2,1,0:T(8,128)(2,1)} %refs_14_.1), custom_call_target="tpu_custom_call" | custom-call | tf_op jit(solution)/shard_map/upper/pallas_call | solution.py:700
  61.0 15.3 %near.1 = (f32[16,16,32,256]{3,2,1,0:T(8,128)}, s32[2,344,128]{2,1,0:T(8,128)}) custom-call(bf16[16,16,32,256]{3,2,1,0:T(8,128)(2,1)} %s_hbm.1, bf16[9,256,256]{2,1,0:T(8,128)(2,1)} %refs_12_.1, s32[256,4,27]{2,1,0:T(4,128)} %bitcast.4, s32[256,4]{1,0:T(8,128)} %bitcast.3, bf16[64,32,128]{2,1,0:T(8,128)(2,1)} %copy-done, bf16[64,32,128]{2,1,0:T(8,128)(2,1)} %copy-done.1), custom_call_target="tpu_custom_call" | custom-call | tf_op jit(solution)/shard_map/near/pallas_call | solution.py:669
  76.3 0.0 collective-permute-done.2.refs_9_
  76.3 0.0 copy-start.3
  76.3 0.0 collective-permute-done.3.refs_10_
  76.3 0.0 copy-start.4
  76.4 0.8 copy-done.3
  77.2 0.3 copy-done.4
  77.4 21.4 %final.1 = bf16[16,16,32,256]{3,2,1,0:T(8,128)(2,1)} custom-call(bf16[5,64,256]{2,1,0:T(8,128)(2,1)} %refs_0_.1, f32[32,256]{1,0:T(8,128)} %upper.1.refs_1_, s32[2,344,128]{2,1,0:T(8,128)} %get-tuple-element.21.refs_2_, bf16[16,8,32,128]{3,2,1,0:T(8,128)(2,1)} %get-tuple-element.22.refs_3_, bf16[8,4,32,128]{3,2,1,0:T(8,128)(2,1)} %get-tuple-element.23.refs_4_, ...), custom_call_target="tpu_custom_call" | custom-call | tf_op jit(solution)/shard_map/final/pallas_call | solution.py:734
  (4 shorter events, 0.0 us)
Async XLA Ops:
  0.0 38.7 %copy-start.5 = (s32[16,16,4]{1,2,0:T(4,128)S(1)}, s32[16,16,4]{1,2,0:T(4,128)}, u32[]{:S(2)}) copy-start(s32[16,16,4]{1,2,0:T(4,128)} %param.15) | copy-start | bytes 12292
  7.1 10.7 %collective-permute-start = (bf16[64,32,128]{2,1,0:T(8,128)(2,1)}, bf16[64,32,128]{2,1,0:T(8,128)(2,1)S(1)}, u32[]{:S(2)}, u32[]{:S(2)}) collective-permute-start(bf16[64,32,128]{2,1,0:T(8,128)(2,1)} %get-tuple-element.19), channel_id=1, source_target_pairs={{0,16},{16,32},{32,48},{48,64},{64,80},{80,96},{96,112},{1,17},{17... | collective-permute-start | bytes 1572872 | tf_op jit(solution)/shard_map/ppermute | solution.py:649
  9.1 10.6 %collective-permute-start.1 = (bf16[64,32,128]{2,1,0:T(8,128)(2,1)}, bf16[64,32,128]{2,1,0:T(8,128)(2,1)S(1)}, u32[]{:S(2)}, u32[]{:S(2)}) collective-permute-start(bf16[64,32,128]{2,1,0:T(8,128)(2,1)} %get-tuple-element.20), channel_id=1, source_target_pairs={{16,0},{32,16},{48,32},{64,48},{80,64},{96,80},{112,96},{17,1},{33... | collective-permute-start | bytes 1572872 | tf_op jit(solution)/shard_map/ppermute | solution.py:650
  17.9 1.9 %copy-start = (bf16[64,32,128]{2,1,0:T(8,128)(2,1)}, bf16[64,32,128]{2,1,0:T(8,128)(2,1)S(1)}, u32[]{:S(2)}) copy-start(bf16[64,32,128]{2,1,0:T(8,128)(2,1)S(1)} %collective-permute-done.lo_hbm.from_lo.refs_7_) | copy-start | bytes 1572868
  19.7 0.8 copy-start.1
  22.2 54.1 %collective-permute-start.2 = (bf16[82,32,128]{2,1,0:T(8,128)(2,1)}, bf16[82,32,128]{2,1,0:T(8,128)(2,1)S(1)}, u32[]{:S(2)}, u32[]{:S(2)}) collective-permute-start(bf16[82,32,128]{2,1,0:T(8,128)(2,1)} %get-tuple-element.28), channel_id=1, source_target_pairs={{0,1},{1,2},{2,3},{3,4},{4,5},{5,6},{6,7},{7,8},{8,9},{9,10},{10,1... | collective-permute-start | bytes 2015240 | tf_op jit(solution)/shard_map/ppermute | solution.py:663
  25.7 50.6 %collective-permute-start.3 = (bf16[82,32,128]{2,1,0:T(8,128)(2,1)}, bf16[82,32,128]{2,1,0:T(8,128)(2,1)S(1)}, u32[]{:S(2)}, u32[]{:S(2)}) collective-permute-start(bf16[82,32,128]{2,1,0:T(8,128)(2,1)} %get-tuple-element.29), channel_id=1, source_target_pairs={{1,0},{2,1},{3,2},{4,3},{5,4},{6,5},{7,6},{8,7},{9,8},{10,9},{11,1... | collective-permute-start | bytes 2015240 | tf_op jit(solution)/shard_map/ppermute | solution.py:664
  28.1 27.9 %all-to-all-start = ((bf16[128,16,128]{2,1,0:T(8,128)(2,1)}), bf16[128,16,128]{2,1,0:T(8,128)(2,1)S(1)}, u32[]{:S(2)}, u32[]{:S(2)}) async-start(bf16[128,16,128]{2,1,0:T(8,128)(2,1)} %get-tuple-element.18), calls=%async_computation | async-start | bytes 1048576 | tf_op jit(solution)/shard_map/all_to_all | solution.py:651
  55.9 0.8 copy-start.2
  76.3 0.8 copy-start.3
  76.3 1.1 %copy-start.4 = (bf16[82,32,128]{2,1,0:T(8,128)(2,1)}, bf16[82,32,128]{2,1,0:T(8,128)(2,1)S(1)}, u32[]{:S(2)}) copy-start(bf16[82,32,128]{2,1,0:T(8,128)(2,1)S(1)} %collective-permute-done.3.refs_10_) | copy-start | bytes 2015236

commit v3 on v2

--- a/solution.py
+++ b/solution.py
@@ -206,7 +206,7 @@
 
 def near_kernel(
     s_hbm, tiles_hbm, codes_hbm, counts_hbm, lo_hbm, hi_hbm, acc_hbm, words_hbm,
-    s_ref, acc_ref, w_ref, tiles_ref, words_ref, codes_ref, counts_ref, lo_ref, hi_ref,
+    s_ref, acc_ref, tiles_ref, words_ref, codes_ref, counts_ref, lo_ref, hi_ref,
     in_sems, out_sems, more_sems,
 ):
     patch = s_ref.shape[0]
@@ -222,15 +222,54 @@
         fetch(i).start()
         return carry
 
-    pairs = [(codes_hbm, codes_ref), (counts_hbm, counts_ref), (lo_hbm, lo_ref), (hi_hbm, hi_ref)]
-    more = [pltpu.make_async_copy(a, b, more_sems.at[2 + k]) for k, (a, b) in enumerate(pairs)]
-    for copy in more:
-        copy.start()
     fetch_tiles = pltpu.make_async_copy(tiles_hbm, tiles_ref, more_sems.at[0])
     put_words = pltpu.make_async_copy(words_ref, words_hbm, more_sems.at[1])
+    pairs = [(lo_hbm, lo_ref), (hi_hbm, hi_ref), (codes_hbm, codes_ref), (counts_hbm, counts_ref)]
+    more = [pltpu.make_async_copy(a, b, more_sems.at[2 + k]) for k, (a, b) in enumerate(pairs)]
+    more[0].start()
     fetch_tiles.start()
     lax.fori_loop(0, patch, start_fetch, 0)
-    for copy in more:
+    for copy in more[1:]:
+        copy.start()
+    fetch_tiles.wait()
+    zeros = jnp.zeros((VEC, 256), BF)
+
+    def shifted(value):
+        return [
+            jnp.concatenate([zeros, value[:-VEC]], 0),
+            value,
+            jnp.concatenate([value[VEC:], zeros], 0),
+        ]
+
+    def put(i, rows):
+        blocks = [
+            r if getattr(r, "ndim", 0) == 2 else s_ref[r].reshape(patch * VEC, 256) for r in rows
+        ]
+        lhs = []
+        for d in range(3):
+            for upper, lower in zip(shifted(blocks[d]), shifted(blocks[d + 1])):
+                lhs.append(jnp.concatenate([upper, lower], 0))
+        tiles = jnp.concatenate([tiles_ref[k] for k in range(9)], 1)
+        out = dot_nt(jnp.concatenate(lhs, 1), tiles)
+        acc_ref[pl.ds(i, 2)] = out.astype(BF).reshape(2, patch, VEC, 256)
+
+    more[0].wait()
+    for i in range(3):
+        fetch(i).wait()
+    cells = {unit[1:]: k for k, unit in enumerate(gx_units(half_sizes(patch), patch)) if unit[0] == "s"}
+
+    def halo_row(ref):
+        return jnp.concatenate(
+            [
+                jnp.concatenate([ref[cells[(j, half)]] for j in range(patch)], 0)
+                for half in range(2)
+            ],
+            1,
+        )
+
+    put(0, [halo_row(lo_ref), 0, 1, 2])
+    put_out(0).start()
+    for copy in more[1:]:
         copy.wait()
     levels = counts_ref.shape[1]
     at = 0
@@ -251,44 +290,6 @@
                     words_ref[group, k : k + 1] = word[r : r + 1]
         at += n * n
     put_words.start()
-    fetch_tiles.wait()
-    for k in range(9):
-        w_ref[k * 256 : k * 256 + 256] = tiles_ref[k].T
-    zeros = jnp.zeros((VEC, 256), BF)
-
-    def shifted(value):
-        return [
-            jnp.concatenate([zeros, value[:-VEC]], 0),
-            value,
-            jnp.concatenate([value[VEC:], zeros], 0),
-        ]
-
-    def put(i, rows):
-        blocks = [
-            r if getattr(r, "ndim", 0) == 2 else s_ref[r].reshape(patch * VEC, 256) for r in rows
-        ]
-        lhs = []
-        for d in range(3):
-            for upper, lower in zip(shifted(blocks[d]), shifted(blocks[d + 1])):
-                lhs.append(jnp.concatenate([upper, lower], 0))
-        out = dot_nn(jnp.concatenate(lhs, 1), w_ref[...])
-        acc_ref[pl.ds(i, 2)] = out.reshape(2, patch, VEC, 256)
-
-    for i in range(3):
-        fetch(i).wait()
-    cells = {unit[1:]: k for k, unit in enumerate(gx_units(half_sizes(patch), patch)) if unit[0] == "s"}
-
-    def halo_row(ref):
-        return jnp.concatenate(
-            [
-                jnp.concatenate([ref[cells[(j, half)]] for j in range(patch)], 0)
-                for half in range(2)
-            ],
-            1,
-        )
-
-    put(0, [halo_row(lo_ref), 0, 1, 2])
-    put_out(0).start()
 
     def row(k, carry):
         i = 2 * k
@@ -446,12 +447,14 @@
             coupling_hbm.at[level], coupling_ref.at[level], level_sems.at[level]
         )
 
-    for k in range(11):
+    first = (9, 10, 12)
+    for k in first:
         fetch(k).start()
+    for k in range(n_in - 1):
+        if k not in first:
+            fetch(k).start()
     for level in (3, 2, 1, 0):
         fetch_level(level).start()
-    for k in range(11, n_in - 1):
-        fetch(k).start()
 
     def start_acc(i, carry):
         fetch_acc(i).start()
@@ -473,25 +476,10 @@
             return coupling_ref[level, d, :, bp * 128 : bp * 128 + 128]
         return shifted[level, d, :, bp * 128 : bp * 128 + 128]
 
-    for k in range(11):
+    for k in first:
         fetch(k).wait()
-    for level in range(4):
-        n = sizes[level]
-        es[level][2 : n + 2, 1 : n // 2 + 1] = qs[level][...]
-    for number, unit in enumerate(gx_units(sizes, patch)):
-        if unit[0] == "q":
-            _, level, r, p = unit
-            es[level][r, p + 1] = from_lo[number]
-            es[level][sizes[level] + 2 + r, p + 1] = from_hi[number]
     starts, base, total = gy_starts(sizes, patch)
     for side, ref in ((0, from_left), (1, from_right)):
-        for level in range(4):
-            n = sizes[level]
-            p = 0 if side == 0 else n // 2 + 1
-            es[level][0:2, p] = ref[2 * level : 2 * level + 2]
-            es[level][2 : n + 2, p] = ref[EDGE + starts[level] : EDGE + starts[level] + n]
-            hi = EDGE + total
-            es[level][n + 2 : n + 4, p] = ref[hi + 2 * level : hi + 2 * level + 2]
         for half in range(2):
             c = slice(half * 128, half * 128 + 128)
             cols[side, 0, :, c] = ref[8 + half]
@@ -533,6 +521,33 @@
         z = jnp.zeros_like(t)
         return [jnp.concatenate([t, z], 0), jnp.concatenate([z, t], 0)]
 
+    for side in range(2):
+        lhs = jnp.concatenate(
+            [cols[side, d : d + patch].reshape(patch * VEC, 256) for d in range(3)], 1
+        )
+        rhs = jnp.concatenate([tiles_ref[3 * d + 2 * side] for d in range(3)], 1)
+        edge_col[side] = dot_nt(lhs, rhs).reshape(patch, VEC, 256)
+
+    for k in range(n_in - 1):
+        if k not in first:
+            fetch(k).wait()
+    for level in range(4):
+        n = sizes[level]
+        es[level][2 : n + 2, 1 : n // 2 + 1] = qs[level][...]
+    for number, unit in enumerate(gx_units(sizes, patch)):
+        if unit[0] == "q":
+            _, level, r, p = unit
+            es[level][r, p + 1] = from_lo[number]
+            es[level][sizes[level] + 2 + r, p + 1] = from_hi[number]
+    starts, base, total = gy_starts(sizes, patch)
+    for side, ref in ((0, from_left), (1, from_right)):
+        for level in range(4):
+            n = sizes[level]
+            p = 0 if side == 0 else n // 2 + 1
+            es[level][0:2, p] = ref[2 * level : 2 * level + 2]
+            es[level][2 : n + 2, p] = ref[EDGE + starts[level] : EDGE + starts[level] + n]
+            hi = EDGE + total
+            es[level][n + 2 : n + 4, p] = ref[hi + 2 * level : hi + 2 * level + 2]
     lax.fori_loop(0, patch, start_acc, 0)
     for level in (3, 2, 1, 0):
         get_level(level)
@@ -558,20 +573,6 @@
     descend(2, b3, b2, [0, 1])
     descend(1, b2, b1, list(range(sizes[1] // 2)))
 
-    def loop0(k, carry):
-        descend(0, b1, b0, [2 * k, 2 * k + 1])
-        return carry
-
-    lax.fori_loop(0, sizes[0] // 4, loop0, 0)
-
-    for k in range(11, n_in - 1):
-        fetch(k).wait()
-    for side in range(2):
-        lhs = jnp.concatenate(
-            [cols[side, d : d + patch].reshape(patch * VEC, 256) for d in range(3)], 1
-        )
-        rhs = jnp.concatenate([tiles_ref[3 * d + 2 * side] for d in range(3)], 1)
-        edge_col[side] = dot_nt(lhs, rhs).reshape(patch, VEC, 256)
     basis = basis_ref[...]
     zb = jnp.zeros_like(basis)
     basis_pair = [jnp.concatenate([basis, zb], 0), jnp.concatenate([zb, basis], 0)]
@@ -583,7 +584,7 @@
         fetch_acc(i).wait()
         value = b0[i].reshape(patch // 2 * VEC, 128)
         far = [dot_nn(value, rhs).reshape(patch // 2, 1, VEC, 256) for rhs in basis_pair]
-        total_row = jnp.concatenate(far, 1).reshape(patch, VEC, 256) + acc_ref[i]
+        total_row = jnp.concatenate(far, 1).reshape(patch, VEC, 256) + acc_ref[i].astype(F32)
         first = total_row[0:1] + edge_col[0, pl.ds(i, 1)]
         last = total_row[patch - 1 : patch] + edge_col[1, pl.ds(i, 1)]
         total_row = jnp.concatenate([first, total_row[1 : patch - 1], last], 0)
@@ -591,7 +592,11 @@
         copy(i).start()
         return carry
 
-    lax.fori_loop(0, patch, finish, 0)
+    def loop0(k, carry):
+        descend(0, b1, b0, [2 * k, 2 * k + 1])
+        return lax.fori_loop(4 * k, 4 * k + 4, finish, carry)
+
+    lax.fori_loop(0, sizes[0] // 4, loop0, 0)
 
     def loop_wait(i, carry):
         copy(i).wait()
@@ -669,15 +674,14 @@
     acc, words = pl.pallas_call(
         near_kernel,
         out_shape=[
-            jax.ShapeDtypeStruct((patch, patch, VEC, 256), F32),
+            jax.ShapeDtypeStruct((patch, patch, VEC, 256), BF),
             jax.ShapeDtypeStruct((2, n_words, 128), jnp.int32),
         ],
         in_specs=[anywhere] * 6,
         out_specs=[anywhere, anywhere],
         scratch_shapes=[
             pltpu.VMEM((patch, patch, VEC, 256), BF),
-            pltpu.VMEM((patch, patch, VEC, 256), F32),
-            pltpu.VMEM((9 * 256, 256), BF),
+            pltpu.VMEM((patch, patch, VEC, 256), BF),
             pltpu.VMEM(near_tiles.shape, BF),
             pltpu.VMEM((2, n_words, 128), jnp.int32),
             pltpu.VMEM(codes.shape, codes.dtype),

time: 99.2 us -> 99 us (level)
  no operation moved by 1% of the time
where the time goes in v3:
time: 99 us; the launch traced here: 98.6 us
  Pallas kernels  49.6 us (50%)
  waiting for transfers between devices  23.3 us (24%)
  starting transfers between devices  22.1 us (22%)
  local copies, waits for them, and re-layouts  3.52 us (4%)
    pallas_call x1, Pallas kernels, shards(): pl.pallas_call(final_kernel, out_shape=jax.ShapeDtypeStruct((patch, patch...  21.3 us
    all_to_all x1, waiting for transfers between devices, shards(): every = lax.all_to_all(q4, ('gx', 'gy'), 0, 0, tiled=True)  16.3 us
    pallas_call x1, Pallas kernels, shards(): pl.pallas_call(near_kernel, out_shape=[jax.ShapeDtypeStruct((patch, patch...  15.1 us
    all_to_all x1, starting transfers between devices, shards(): every = lax.all_to_all(q4, ('gx', 'gy'), 0, 0, tiled=True)  10.7 us
    pallas_call x1, Pallas kernels, shards(): pl.pallas_call(project_kernel, out_shape=[jax.ShapeDtypeStruct(v, BF) for...  7.16 us
    ppermute x1, waiting for transfers between devices, shards(): from_lo = lax.ppermute(gx_hi, 'gx', up(n_gx))  5.13 us
    pallas_call x1, Pallas kernels, shards(): pl.pallas_call(upper_kernel, out_shape=jax.ShapeDtypeStruct((VEC, transfe...  4.3 us
    ppermute x1, starting transfers between devices, shards(): from_hi = lax.ppermute(gx_lo, 'gx', dn(n_gx))  3.64 us
  transfers between devices with their start and end apart: 5, of which 3 were waited for; matrix products, arithmetic and copies ran while one was open for 1% of the time, Pallas kernels for 20%

profile of v3, /device:TPU:28, one launch (start us, length us, event | category | flops | bytes accessed | tf_op | source)
XLA Modules:
  0.0 98.6 jit_solution(4715649070306921486)
XLA Ops:
  0.0 7.2 %project.1 = (bf16[16,8,32,128]{3,2,1,0:T(8,128)(2,1)}, bf16[8,4,32,128]{3,2,1,0:T(8,128)(2,1)}, bf16[4,2,32,128]{3,2,1,0:T(8,128)(2,1)}, bf16[2,1,32,128]{3,2,1...) custom-call(bf16[16,16,32,256]{3,2,1,0:T(8,128)(2,1)} %s_hbm.1, ...), custom_call_target="tpu_custom_call" | custom-call | tf_op jit(solution)/shard_map/project/pallas_call | solution.py:632
  7.2 1.9 %collective-permute-start = (bf16[64,32,128]{2,1,0:T(8,128)(2,1)}, bf16[64,32,128]{2,1,0:T(8,128)(2,1)S(1)}, u32[]{:S(2)}, u32[]{:S(2)}) collective-permute-start(bf16[64,32,128]{2,1,0:T(8,128)(2,1)} %get-tuple-element.19), channel_id=1, source_target_pairs={{0,16},{16,32},{32,48},{48,64},{64,80},{80,96},{96,112},{1,17},{17... | collective-permute-start | bytes 1572872 | tf_op jit(solution)/shard_map/ppermute | solution.py:654
  9.1 3.6 %collective-permute-start.1 = (bf16[64,32,128]{2,1,0:T(8,128)(2,1)}, bf16[64,32,128]{2,1,0:T(8,128)(2,1)S(1)}, u32[]{:S(2)}, u32[]{:S(2)}) collective-permute-start(bf16[64,32,128]{2,1,0:T(8,128)(2,1)} %get-tuple-element.20), channel_id=1, source_target_pairs={{16,0},{32,16},{48,32},{64,48},{80,64},{96,80},{112,96},{17,1},{33... | collective-permute-start | bytes 1572872 | tf_op jit(solution)/shard_map/ppermute | solution.py:655
  12.7 5.1 %collective-permute-done.lo_hbm.from_lo.refs_7_ = bf16[64,32,128]{2,1,0:T(8,128)(2,1)S(1)} collective-permute-done((bf16[64,32,128]{2,1,0:T(8,128)(2,1)}, bf16[64,32,128]{2,1,0:T(8,128)(2,1)S(1)}, u32[]{:S(2)}, u32[]{:S(2)}) %collective-permute-start) | collective-permute-done | bytes 524320 | tf_op jit(solution)/shard_map/ppermute | solution.py:654
  17.9 1.9 %collective-permute-done.1.hi_hbm.from_hi.refs_8_ = bf16[64,32,128]{2,1,0:T(8,128)(2,1)S(1)} collective-permute-done((bf16[64,32,128]{2,1,0:T(8,128)(2,1)}, bf16[64,32,128]{2,1,0:T(8,128)(2,1)S(1)}, u32[]{:S(2)}, u32[]{:S(2)}) %collective-permute-start.1) | collective-permute-done | bytes 524320 | tf_op jit(solution)/shard_map/ppermute | solution.py:655
  19.7 0.0 copy-done
  19.7 0.8 copy-done.1
  20.5 1.7 %corner.1 = (bf16[82,32,128]{2,1,0:T(8,128)(2,1)}, bf16[82,32,128]{2,1,0:T(8,128)(2,1)}) custom-call(bf16[64,32,128]{2,1,0:T(8,128)(2,1)} %copy-done, bf16[64,32,128]{2,1,0:T(8,128)(2,1)} %copy-done.1, bf16[82,32,128]{2,1,0:T(8,128)(2,1)} %get-tuple-element.26.left_in, ...), custom_call_target="tpu_custom_call", output_to_operand_aliasing={{0}: (2, {}), {1}: (3, {})} | custom-call | tf_op jit(solution)/shard_map/corner/pallas_call | solution.py:658
  22.2 3.5 %collective-permute-start.2 = (bf16[82,32,128]{2,1,0:T(8,128)(2,1)}, bf16[82,32,128]{2,1,0:T(8,128)(2,1)S(1)}, u32[]{:S(2)}, u32[]{:S(2)}) collective-permute-start(bf16[82,32,128]{2,1,0:T(8,128)(2,1)} %get-tuple-element.28), channel_id=1, source_target_pairs={{0,1},{1,2},{2,3},{3,4},{4,5},{5,6},{6,7},{7,8},{8,9},{9,10},{10,1... | collective-permute-start | bytes 2015240 | tf_op jit(solution)/shard_map/ppermute | solution.py:668
  25.7 2.4 %collective-permute-start.3 = (bf16[82,32,128]{2,1,0:T(8,128)(2,1)}, bf16[82,32,128]{2,1,0:T(8,128)(2,1)S(1)}, u32[]{:S(2)}, u32[]{:S(2)}) collective-permute-start(bf16[82,32,128]{2,1,0:T(8,128)(2,1)} %get-tuple-element.29), channel_id=1, source_target_pairs={{1,0},{2,1},{3,2},{4,3},{5,4},{6,5},{7,6},{8,7},{9,8},{10,9},{11,1... | collective-permute-start | bytes 2015240 | tf_op jit(solution)/shard_map/ppermute | solution.py:669
  28.1 10.7 %all-to-all-start = ((bf16[128,16,128]{2,1,0:T(8,128)(2,1)}), bf16[128,16,128]{2,1,0:T(8,128)(2,1)S(1)}, u32[]{:S(2)}, u32[]{:S(2)}) async-start(bf16[128,16,128]{2,1,0:T(8,128)(2,1)} %get-tuple-element.18), calls=%async_computation | async-start | bytes 1048576 | tf_op jit(solution)/shard_map/all_to_all | solution.py:656
  38.8 0.0 copy-done.5
  38.8 0.8 copy.12
  39.6 16.3 %all-to-all-done.every_hbm = bf16[128,16,128]{2,1,0:T(8,128)(2,1)S(1)} async-done(((bf16[128,16,128]{2,1,0:T(8,128)(2,1)}), bf16[128,16,128]{2,1,0:T(8,128)(2,1)S(1)}, u32[]{:S(2)}, u32[]{:S(2)}) %all-to-all-start) | async-done | bytes 524320 | tf_op jit(solution)/shard_map/all_to_all | solution.py:656
  56.0 0.8 copy-done.2
  56.8 4.3 %upper.1.refs_1_ = f32[32,256]{1,0:T(8,128)} custom-call(s32[168]{0:T(256)} %counts_upper_ref.1, s32[27,168]{1,0:T(8,128)} %bitcast.5, bf16[128,16,128]{2,1,0:T(8,128)(2,1)} %copy-done.2, bf16[5,64,256]{2,1,0:T(8,128)(2,1)} %refs_0_.1, bf16[5,7,64,448]{3,2,1,0:T(8,128)(2,1)} %refs_14_.1), custom_call_target="tpu_custom_call" | custom-call | tf_op jit(solution)/shard_map/upper/pallas_call | solution.py:704
  61.1 15.1 %near.1 = (bf16[16,16,32,256]{3,2,1,0:T(8,128)(2,1)}, s32[2,344,128]{2,1,0:T(8,128)}) custom-call(bf16[16,16,32,256]{3,2,1,0:T(8,128)(2,1)} %s_hbm.1, bf16[9,256,256]{2,1,0:T(8,128)(2,1)} %refs_12_.1, s32[256,4,27]{2,1,0:T(4,128)} %bitcast.4, s32[256,4]{1,0:T(8,128)} %bitcast.3, bf16[64,32,128]{2,1,0:T(8,128)(2,1)} %copy-done, bf16[64,32,128]{2,1,0:T(8,128)(2,1)} %copy-done.1), custom_call_target="tpu_custom_call" | custom-call | tf_op jit(solution)/shard_map/near/pallas_call | solution.py:674
  76.2 0.0 collective-permute-done.2.refs_9_
  76.2 0.0 copy-start.3
  76.2 0.0 collective-permute-done.3.refs_10_
  76.3 0.0 copy-start.4
  76.3 0.8 copy-done.3
  77.1 0.3 copy-done.4
  77.4 21.3 %final.1 = bf16[16,16,32,256]{3,2,1,0:T(8,128)(2,1)} custom-call(bf16[5,64,256]{2,1,0:T(8,128)(2,1)} %refs_0_.1, f32[32,256]{1,0:T(8,128)} %upper.1.refs_1_, s32[2,344,128]{2,1,0:T(8,128)} %get-tuple-element.21.refs_2_, bf16[16,8,32,128]{3,2,1,0:T(8,128)(2,1)} %get-tuple-element.22.refs_3_, bf16[8,4,32,128]{3,2,1,0:T(8,128)(2,1)} %get-tuple-element.23.refs_4_, ...), custom_call_target="tpu_custom_call" | custom-call | tf_op jit(solution)/shard_map/final/pallas_call | solution.py:738
  (4 shorter events, 0.0 us)
Async XLA Ops:
  0.0 38.8 %copy-start.5 = (s32[16,16,4]{1,2,0:T(4,128)S(1)}, s32[16,16,4]{1,2,0:T(4,128)}, u32[]{:S(2)}) copy-start(s32[16,16,4]{1,2,0:T(4,128)} %param.15) | copy-start | bytes 12292
  7.2 10.7 %collective-permute-start = (bf16[64,32,128]{2,1,0:T(8,128)(2,1)}, bf16[64,32,128]{2,1,0:T(8,128)(2,1)S(1)}, u32[]{:S(2)}, u32[]{:S(2)}) collective-permute-start(bf16[64,32,128]{2,1,0:T(8,128)(2,1)} %get-tuple-element.19), channel_id=1, source_target_pairs={{0,16},{16,32},{32,48},{48,64},{64,80},{80,96},{96,112},{1,17},{17... | collective-permute-start | bytes 1572872 | tf_op jit(solution)/shard_map/ppermute | solution.py:654
  9.1 10.6 %collective-permute-start.1 = (bf16[64,32,128]{2,1,0:T(8,128)(2,1)}, bf16[64,32,128]{2,1,0:T(8,128)(2,1)S(1)}, u32[]{:S(2)}, u32[]{:S(2)}) collective-permute-start(bf16[64,32,128]{2,1,0:T(8,128)(2,1)} %get-tuple-element.20), channel_id=1, source_target_pairs={{16,0},{32,16},{48,32},{64,48},{80,64},{96,80},{112,96},{17,1},{33... | collective-permute-start | bytes 1572872 | tf_op jit(solution)/shard_map/ppermute | solution.py:655
  17.9 1.9 %copy-start = (bf16[64,32,128]{2,1,0:T(8,128)(2,1)}, bf16[64,32,128]{2,1,0:T(8,128)(2,1)S(1)}, u32[]{:S(2)}) copy-start(bf16[64,32,128]{2,1,0:T(8,128)(2,1)S(1)} %collective-permute-done.lo_hbm.from_lo.refs_7_) | copy-start | bytes 1572868
  19.7 0.8 copy-start.1
  22.2 54.0 %collective-permute-start.2 = (bf16[82,32,128]{2,1,0:T(8,128)(2,1)}, bf16[82,32,128]{2,1,0:T(8,128)(2,1)S(1)}, u32[]{:S(2)}, u32[]{:S(2)}) collective-permute-start(bf16[82,32,128]{2,1,0:T(8,128)(2,1)} %get-tuple-element.28), channel_id=1, source_target_pairs={{0,1},{1,2},{2,3},{3,4},{4,5},{5,6},{6,7},{7,8},{8,9},{9,10},{10,1... | collective-permute-start | bytes 2015240 | tf_op jit(solution)/shard_map/ppermute | solution.py:668
  25.7 50.5 %collective-permute-start.3 = (bf16[82,32,128]{2,1,0:T(8,128)(2,1)}, bf16[82,32,128]{2,1,0:T(8,128)(2,1)S(1)}, u32[]{:S(2)}, u32[]{:S(2)}) collective-permute-start(bf16[82,32,128]{2,1,0:T(8,128)(2,1)} %get-tuple-element.29), channel_id=1, source_target_pairs={{1,0},{2,1},{3,2},{4,3},{5,4},{6,5},{7,6},{8,7},{9,8},{10,9},{11,1... | collective-permute-start | bytes 2015240 | tf_op jit(solution)/shard_map/ppermute | solution.py:669
  28.1 27.9 %all-to-all-start = ((bf16[128,16,128]{2,1,0:T(8,128)(2,1)}), bf16[128,16,128]{2,1,0:T(8,128)(2,1)S(1)}, u32[]{:S(2)}, u32[]{:S(2)}) async-start(bf16[128,16,128]{2,1,0:T(8,128)(2,1)} %get-tuple-element.18), calls=%async_computation | async-start | bytes 1048576 | tf_op jit(solution)/shard_map/all_to_all | solution.py:656
  56.0 0.8 copy-start.2
  76.2 0.9 copy-start.3
  76.3 1.1 %copy-start.4 = (bf16[82,32,128]{2,1,0:T(8,128)(2,1)}, bf16[82,32,128]{2,1,0:T(8,128)(2,1)S(1)}, u32[]{:S(2)}) copy-start(bf16[82,32,128]{2,1,0:T(8,128)(2,1)S(1)} %collective-permute-done.3.refs_10_) | copy-start | bytes 2015236

commit v4 on v3

--- a/solution.py
+++ b/solution.py
@@ -193,6 +193,15 @@
     return words
 
 
+def column(table):
+    n, m = table.shape
+    wide = jnp.broadcast_to(table[:, None, :], (n, m, m))
+    row = lax.broadcasted_iota(jnp.int32, (n, m, m), 1)
+    lane = lax.broadcasted_iota(jnp.int32, (n, m, m), 2)
+    picked = jnp.where(row == lane, wide, 0).astype(F32)
+    return jnp.sum(picked.reshape(n * m, m), axis=1, keepdims=True).astype(jnp.int32)
+
+
 def half_sizes(patch):
     return [patch // 2**k for k in range(4)]
 
@@ -275,7 +284,7 @@
     at = 0
     for level in range(levels):
         n = patch >> level
-        counts = counts_ref[:, level : level + 1]
+        counts = column(counts_ref[:, level, :])
         codes = codes_ref[:, level, :]
         for group, power in enumerate(list_words(codes, counts)):
             word = jnp.sum(power, axis=1, keepdims=True).astype(jnp.int32)
@@ -334,21 +343,68 @@
     return jnp.concatenate([m, m, m, m], 0).astype(BF)
 
 
-def upper_kernel(
-    counts_upper_ref, codes_upper_ref, every_hbm, transfer_hbm, coupling_hbm, out_ref,
-    every, transfer_ref, coupling_ref, shifted, f4, f5, f6, sems,
+def final_kernel(
+    counts_upper_ref, codes_upper_ref, *refs,
 ):
-    pairs = [(every_hbm, every), (transfer_hbm, transfer_ref)]
-    pairs += [(coupling_hbm.at[coupling_hbm.shape[0] - 1], coupling_ref)]
-    copies = [pltpu.make_async_copy(a, b, sems.at[k]) for k, (a, b) in enumerate(pairs)]
-    for copy in copies:
-        copy.start()
+    n_in = 14
+    sources, coupling_hbm, out_ref = refs[:n_in], refs[n_in], refs[n_in + 1]
+    buffers, rest = refs[n_in + 2 : 2 * n_in + 2], refs[2 * n_in + 2 :]
+    (
+        transfer_ref, every, words_ref, q0, q1, q2, q3,
+        from_lo, from_hi, from_left, from_right, basis_ref, tiles_ref, acc_ref,
+    ) = buffers
+    (
+    e0, e1, e2, e3, f4, f5, f6, shifted, b0, b1, b2, b3, cols, edge_col, out_buf, coupling_ref,
+    sems, in_sems, acc_sems, level_sems,
+    ) = rest
+    patch = acc_ref.shape[0]
+
+    def fetch(k):
+        return pltpu.make_async_copy(sources[k], buffers[k], in_sems.at[k])
+
+    def fetch_acc(i):
+        return pltpu.make_async_copy(sources[n_in - 1].at[i], acc_ref.at[i], acc_sems.at[i])
+
+    def fetch_level(level):
+        return pltpu.make_async_copy(
+            coupling_hbm.at[level], coupling_ref.at[level], level_sems.at[level]
+        )
+
+    first = (9, 10, 12)
+    fetch(1).start()
+    fetch(0).start()
+    fetch_level(4).start()
+    for k in first:
+        fetch(k).start()
+    for k in range(2, n_in - 1):
+        if k not in first:
+            fetch(k).start()
+    for level in (3, 2, 1, 0):
+        fetch_level(level).start()
+
+    def start_acc(i, carry):
+        fetch_acc(i).start()
+        return carry
+
+    qs = [q0, q1, q2, q3]
+    es = [e0, e1, e2, e3]
+    sizes = [q.shape[0] for q in qs]
     lanes = lane_bits()
-    for copy in copies:
-        copy.wait()
-    for d in range(7):
-        shifted[d] = coupling_ref[d, :, 64:448]
-
+    word_at = word_offsets(sizes)
+
+    def get_level(level):
+        fetch_level(level).wait()
+        for d in range(7):
+            shifted[level, d] = coupling_ref[level, d, :, 64:448]
+
+    def block(level, col_bit, d, bp):
+        if col_bit == 1:
+            return coupling_ref[level, d, :, bp * 128 : bp * 128 + 128]
+        return shifted[level, d, :, bp * 128 : bp * 128 + 128]
+
+    fetch(0).wait()
+    fetch(1).wait()
+    get_level(4)
     f4[...] = jnp.zeros_like(f4)
     f5[...] = jnp.zeros_like(f5)
     f6[...] = jnp.zeros_like(f6)
@@ -405,8 +461,8 @@
         for a in range(6):
             for bp in range(3):
                 lhs.append(f[top_row + a, left + bp] * mask_of(words, a, bp, lanes))
-            even = shifted[a + 1 - rb]
-            odd = coupling_ref[a + 1 - rb][:, 0:384]
+            even = shifted[4, a + 1 - rb]
+            odd = coupling_ref[4, a + 1 - rb][:, 0:384]
             rhs.append(jnp.where(cb == 1, odd, even))
         uppers.append(dot_nt(jnp.concatenate(lhs, 1), jnp.concatenate(rhs, 1)))
     down = uppers[-1]
@@ -417,64 +473,7 @@
         half = jnp.where((r_here & 1) == 1, carried[:, 128:256], carried[:, 0:128])
         half = jnp.where((c_here & 1) == 1, pltpu.roll(half, 64, 1), half)
         down = uppers[step] + half[:, 0:64]
-    out_ref[...] = dot_nn(down.astype(BF), transfer_ref[3])
-
-
-def final_kernel(
-    *refs,
-):
-    n_in = 14
-    sources, coupling_hbm, out_ref = refs[:n_in], refs[n_in], refs[n_in + 1]
-    buffers, rest = refs[n_in + 2 : 2 * n_in + 2], refs[2 * n_in + 2 :]
-    (
-        transfer_ref, carried_ref, words_ref, q0, q1, q2, q3,
-        from_lo, from_hi, from_left, from_right, basis_ref, tiles_ref, acc_ref,
-    ) = buffers
-    (
-    e0, e1, e2, e3, shifted, b0, b1, b2, b3, cols, edge_col, out_buf, coupling_ref,
-    sems, in_sems, acc_sems, level_sems,
-    ) = rest
-    patch = acc_ref.shape[0]
-
-    def fetch(k):
-        return pltpu.make_async_copy(sources[k], buffers[k], in_sems.at[k])
-
-    def fetch_acc(i):
-        return pltpu.make_async_copy(sources[n_in - 1].at[i], acc_ref.at[i], acc_sems.at[i])
-
-    def fetch_level(level):
-        return pltpu.make_async_copy(
-            coupling_hbm.at[level], coupling_ref.at[level], level_sems.at[level]
-        )
-
-    first = (9, 10, 12)
-    for k in first:
-        fetch(k).start()
-    for k in range(n_in - 1):
-        if k not in first:
-            fetch(k).start()
-    for level in (3, 2, 1, 0):
-        fetch_level(level).start()
-
-    def start_acc(i, carry):
-        fetch_acc(i).start()
-        return carry
-
-    qs = [q0, q1, q2, q3]
-    es = [e0, e1, e2, e3]
-    sizes = [q.shape[0] for q in qs]
-    lanes = lane_bits()
-    word_at = word_offsets(sizes)
-
-    def get_level(level):
-        fetch_level(level).wait()
-        for d in range(7):
-            shifted[level, d] = coupling_ref[level, d, :, 64:448]
-
-    def block(level, col_bit, d, bp):
-        if col_bit == 1:
-            return coupling_ref[level, d, :, bp * 128 : bp * 128 + 128]
-        return shifted[level, d, :, bp * 128 : bp * 128 + 128]
+    carried3 = dot_nn(down.astype(BF), transfer_ref[3])
 
     for k in first:
         fetch(k).wait()
@@ -528,7 +527,7 @@
         rhs = jnp.concatenate([tiles_ref[3 * d + 2 * side] for d in range(3)], 1)
         edge_col[side] = dot_nt(lhs, rhs).reshape(patch, VEC, 256)
 
-    for k in range(n_in - 1):
+    for k in range(2, n_in - 1):
         if k not in first:
             fetch(k).wait()
     for level in range(4):
@@ -551,7 +550,6 @@
     lax.fori_loop(0, patch, start_acc, 0)
     for level in (3, 2, 1, 0):
         get_level(level)
-    carried3 = carried_ref[...]
     for row_bit in range(2):
         u = images(3, [0], row_bit)
         b3[row_bit, 0] = (u + carried3[:, row_bit * 128 : row_bit * 128 + 128]).astype(BF)
@@ -670,7 +668,7 @@
 
     n_words = -(-word_offsets(sizes)[-1] // 8) * 8
     codes = codes_local.reshape(patch * patch, *codes_local.shape[2:])
-    counts = counts_local.reshape(patch * patch, counts_local.shape[2])
+    counts = counts_local.transpose(0, 2, 1)
     acc, words = pl.pallas_call(
         near_kernel,
         out_shape=[
@@ -701,50 +699,35 @@
     def padded(rows, pairs):
         return pltpu.VMEM((rows + 4, pairs + 2, VEC, 128), BF)
 
-    carried = pl.pallas_call(
-        upper_kernel,
-        out_shape=jax.ShapeDtypeStruct((VEC, transfer.shape[2]), F32),
-        in_specs=[sspec(), vspec()] + [anywhere] * 3,
-        out_specs=vspec(),
-        scratch_shapes=[
-            pltpu.VMEM(every.shape, BF),
-            pltpu.VMEM(transfer.shape, BF),
-            pltpu.VMEM(coupling.shape[1:], BF),
-            pltpu.VMEM((7, RANK, 384), BF),
-        ]
-        + [padded(n_gx // 2**k, n_gy // 2 ** (k + 1)) for k in range(3)]
-        + [pltpu.SemaphoreType.DMA((3,))],
-        compiler_params=params,
-        name="upper",
-    )(counts_upper, codes_upper.T, every, transfer, coupling)
     inputs = [
-        transfer, carried, words, q0, q1, q2, q3,
+        transfer, every, words, q0, q1, q2, q3,
         from_lo, from_hi, from_left, from_right, leaf_basis, near_tiles, acc,
     ]
     scratch = [pltpu.VMEM(v.shape, v.dtype) for v in inputs]
     scratch += [padded(n, n // 2) for n in sizes]
-    scratch += [pltpu.VMEM((4, 7, RANK, 384), BF)]
+    scratch += [padded(n_gx // 2**k, n_gy // 2 ** (k + 1)) for k in range(3)]
+    scratch += [pltpu.VMEM((5, 7, RANK, 384), BF)]
     scratch += [pltpu.VMEM((n, n // 2, VEC, 128), BF) for n in sizes]
     scratch += [
         pltpu.VMEM((2, patch + 2, VEC, 256), BF),
         pltpu.VMEM((2, patch, VEC, 256), F32),
         pltpu.VMEM((patch, patch, VEC, 256), BF),
-        pltpu.VMEM((4, *coupling.shape[1:]), BF),
+        pltpu.VMEM(coupling.shape, BF),
         pltpu.SemaphoreType.DMA((patch,)),
         pltpu.SemaphoreType.DMA((len(inputs) - 1,)),
         pltpu.SemaphoreType.DMA((patch,)),
-        pltpu.SemaphoreType.DMA((4,)),
+        pltpu.SemaphoreType.DMA((5,)),
     ]
     return pl.pallas_call(
         final_kernel,
         out_shape=jax.ShapeDtypeStruct((patch, patch, VEC, 256), BF),
-        in_specs=[anywhere] * (len(inputs) + 1),
+        in_specs=[sspec(), vspec()] + [anywhere] * (len(inputs) + 1),
         out_specs=pl.BlockSpec(memory_space=pl.ANY),
         scratch_shapes=scratch,
         compiler_params=params,
         name="final",
     )(
-        *inputs, coupling,
+        counts_upper, codes_upper.T, *inputs, coupling,
     )
 
 

time: 99 us -> 81.6 us (0.82)
  the two profiles are of different devices: /device:TPU:28 before, /device:TPU:26 now
where the time goes in v4:
time: 81.6 us; the launch traced here: 81.3 us
  Pallas kernels  48 us (59%)
  starting transfers between devices  22.1 us (27%)
  waiting for transfers between devices  8.99 us (11%)
  local copies, waits for them, and re-layouts  2.1 us (3%)
    pallas_call x1, Pallas kernels, shards(): pl.pallas_call(final_kernel, out_shape=jax.ShapeDtypeStruct((patch, patch...  24 us
    pallas_call x1, Pallas kernels, shards(): pl.pallas_call(near_kernel, out_shape=[jax.ShapeDtypeStruct((patch, patch...  15.1 us
    all_to_all x1, starting transfers between devices, shards(): every = lax.all_to_all(q4, ('gx', 'gy'), 0, 0, tiled=True)  10.7 us
    pallas_call x1, Pallas kernels, shards(): pl.pallas_call(project_kernel, out_shape=[jax.ShapeDtypeStruct(v, BF) for...  7.16 us
    ppermute x1, waiting for transfers between devices, shards(): from_lo = lax.ppermute(gx_hi, 'gx', up(n_gx))  5.13 us
    ppermute x1, starting transfers between devices, shards(): from_hi = lax.ppermute(gx_lo, 'gx', dn(n_gx))  3.64 us
    ppermute x1, starting transfers between devices, shards(): from_left = lax.ppermute(send_right, 'gy', up(n_gy))  3.49 us
    ppermute x1, starting transfers between devices, shards(): from_right = lax.ppermute(send_left, 'gy', dn(n_gy))  2.35 us
  transfers between devices with their start and end apart: 5, of which 3 were waited for; matrix products, arithmetic and copies ran while one was open for 0% of the time, Pallas kernels for 19%

profile of v4, /device:TPU:26, one launch (start us, length us, event | category | flops | bytes accessed | tf_op | source)
XLA Modules:
  0.0 81.3 jit_solution(13398672556321429189)
XLA Ops:
  0.0 7.2 %project.1 = (bf16[16,8,32,128]{3,2,1,0:T(8,128)(2,1)}, bf16[8,4,32,128]{3,2,1,0:T(8,128)(2,1)}, bf16[4,2,32,128]{3,2,1,0:T(8,128)(2,1)}, bf16[2,1,32,128]{3,2,1...) custom-call(bf16[16,16,32,256]{3,2,1,0:T(8,128)(2,1)} %s_hbm.1, ...), custom_call_target="tpu_custom_call" | custom-call | tf_op jit(solution)/shard_map/project/pallas_call | solution.py:630
  7.2 1.9 %collective-permute-start = (bf16[64,32,128]{2,1,0:T(8,128)(2,1)}, bf16[64,32,128]{2,1,0:T(8,128)(2,1)S(1)}, u32[]{:S(2)}, u32[]{:S(2)}) collective-permute-start(bf16[64,32,128]{2,1,0:T(8,128)(2,1)} %get-tuple-element.19), channel_id=1, source_target_pairs={{0,16},{16,32},{32,48},{48,64},{64,80},{80,96},{96,112},{1,17},{17... | collective-permute-start | bytes 1572872 | tf_op jit(solution)/shard_map/ppermute | solution.py:652
  9.1 3.6 %collective-permute-start.1 = (bf16[64,32,128]{2,1,0:T(8,128)(2,1)}, bf16[64,32,128]{2,1,0:T(8,128)(2,1)S(1)}, u32[]{:S(2)}, u32[]{:S(2)}) collective-permute-start(bf16[64,32,128]{2,1,0:T(8,128)(2,1)} %get-tuple-element.20), channel_id=1, source_target_pairs={{16,0},{32,16},{48,32},{64,48},{80,64},{96,80},{112,96},{17,1},{33... | collective-permute-start | bytes 1572872 | tf_op jit(solution)/shard_map/ppermute | solution.py:653
  12.7 5.1 %collective-permute-done.lo_hbm.from_lo.refs_7_ = bf16[64,32,128]{2,1,0:T(8,128)(2,1)S(1)} collective-permute-done((bf16[64,32,128]{2,1,0:T(8,128)(2,1)}, bf16[64,32,128]{2,1,0:T(8,128)(2,1)S(1)}, u32[]{:S(2)}, u32[]{:S(2)}) %collective-permute-start) | collective-permute-done | bytes 524320 | tf_op jit(solution)/shard_map/ppermute | solution.py:652
  17.9 0.0 copy-start
  17.9 1.9 %collective-permute-done.1.hi_hbm.from_hi.refs_8_ = bf16[64,32,128]{2,1,0:T(8,128)(2,1)S(1)} collective-permute-done((bf16[64,32,128]{2,1,0:T(8,128)(2,1)}, bf16[64,32,128]{2,1,0:T(8,128)(2,1)S(1)}, u32[]{:S(2)}, u32[]{:S(2)}) %collective-permute-start.1) | collective-permute-done | bytes 524320 | tf_op jit(solution)/shard_map/ppermute | solution.py:653
  19.7 0.0 copy-start.1
  19.7 0.0 copy-done
  19.7 0.8 copy-done.1
  20.5 1.7 %corner.1 = (bf16[82,32,128]{2,1,0:T(8,128)(2,1)}, bf16[82,32,128]{2,1,0:T(8,128)(2,1)}) custom-call(bf16[64,32,128]{2,1,0:T(8,128)(2,1)} %copy-done, bf16[64,32,128]{2,1,0:T(8,128)(2,1)} %copy-done.1, bf16[82,32,128]{2,1,0:T(8,128)(2,1)} %get-tuple-element.26.left_in, ...), custom_call_target="tpu_custom_call", output_to_operand_aliasing={{0}: (2, {}), {1}: (3, {})} | custom-call | tf_op jit(solution)/shard_map/corner/pallas_call | solution.py:656
  22.2 3.5 %collective-permute-start.2 = (bf16[82,32,128]{2,1,0:T(8,128)(2,1)}, bf16[82,32,128]{2,1,0:T(8,128)(2,1)S(1)}, u32[]{:S(2)}, u32[]{:S(2)}) collective-permute-start(bf16[82,32,128]{2,1,0:T(8,128)(2,1)} %get-tuple-element.28), channel_id=1, source_target_pairs={{0,1},{1,2},{2,3},{3,4},{4,5},{5,6},{6,7},{7,8},{8,9},{9,10},{10,1... | collective-permute-start | bytes 2015240 | tf_op jit(solution)/shard_map/ppermute | solution.py:666
  25.7 2.4 %collective-permute-start.3 = (bf16[82,32,128]{2,1,0:T(8,128)(2,1)}, bf16[82,32,128]{2,1,0:T(8,128)(2,1)S(1)}, u32[]{:S(2)}, u32[]{:S(2)}) collective-permute-start(bf16[82,32,128]{2,1,0:T(8,128)(2,1)} %get-tuple-element.29), channel_id=1, source_target_pairs={{1,0},{2,1},{3,2},{4,3},{5,4},{6,5},{7,6},{8,7},{9,8},{10,9},{11,1... | collective-permute-start | bytes 2015240 | tf_op jit(solution)/shard_map/ppermute | solution.py:667
  28.1 10.7 %all-to-all-start = ((bf16[128,16,128]{2,1,0:T(8,128)(2,1)}), bf16[128,16,128]{2,1,0:T(8,128)(2,1)S(1)}, u32[]{:S(2)}, u32[]{:S(2)}) async-start(bf16[128,16,128]{2,1,0:T(8,128)(2,1)} %get-tuple-element.18), calls=%async_computation | async-start | bytes 1048576 | tf_op jit(solution)/shard_map/all_to_all | solution.py:654
  38.8 15.1 %near.1 = (bf16[16,16,32,256]{3,2,1,0:T(8,128)(2,1)}, s32[2,344,128]{2,1,0:T(8,128)}) custom-call(bf16[16,16,32,256]{3,2,1,0:T(8,128)(2,1)} %s_hbm.1, bf16[9,256,256]{2,1,0:T(8,128)(2,1)} %refs_12_.1, s32[256,4,27]{2,1,0:T(4,128)} %bitcast.3, s32[16,4,16]{2,1,0:T(4,128)} %bitcast.4, bf16[64,32,128]{2,1,0:T(8,128)(2,1)} %copy-done, bf16[64,32,128]{2,1,0:T(8,128)(2,1)} %copy-done.1), custom_call_target="tpu_custom_call" | custom-call | tf_op jit(solution)/shard_map/near/pallas_call | solution.py:672
  54.0 2.0 %all-to-all-done.refs_1_ = bf16[128,16,128]{2,1,0:T(8,128)(2,1)S(1)} async-done(((bf16[128,16,128]{2,1,0:T(8,128)(2,1)}), bf16[128,16,128]{2,1,0:T(8,128)(2,1)S(1)}, u32[]{:S(2)}, u32[]{:S(2)}) %all-to-all-start) | async-done | bytes 524320 | tf_op jit(solution)/shard_map/all_to_all | solution.py:654
  56.0 0.0 copy-start.2
  56.0 0.0 collective-permute-done.2.refs_9_
  56.0 0.0 copy-start.3
  56.0 0.0 collective-permute-done.3.refs_10_
  56.0 0.0 copy-start.4
  56.0 0.8 copy-done.2
  56.8 0.3 copy-done.3
  57.0 0.2 copy-done.4
  57.3 24.0 %final.1 = bf16[16,16,32,256]{3,2,1,0:T(8,128)(2,1)} custom-call(s32[168]{0:T(256)} %counts_upper_ref.1, s32[27,168]{1,0:T(8,128)} %bitcast.5, bf16[5,64,256]{2,1,0:T(8,128)(2,1)} %refs_0_.1, bf16[128,16,128]{2,1,0:T(8,128)(2,1)} %copy-done.2, s32[2,344,128]{2,1,0:T(8,128)} %get-tuple-element.21.refs_2_, bf16[16,8,32,128]{3,2,1,0:T(8,128)(2,1)} %get-tuple-element.22.refs_3_, ...), custom_call_target="tpu_custom_call" | custom-call | tf_op jit(solution)/shard_map/final/pallas_call | solution.py:721
Async XLA Ops:
  7.2 10.7 %collective-permute-start = (bf16[64,32,128]{2,1,0:T(8,128)(2,1)}, bf16[64,32,128]{2,1,0:T(8,128)(2,1)S(1)}, u32[]{:S(2)}, u32[]{:S(2)}) collective-permute-start(bf16[64,32,128]{2,1,0:T(8,128)(2,1)} %get-tuple-element.19), channel_id=1, source_target_pairs={{0,16},{16,32},{32,48},{48,64},{64,80},{80,96},{96,112},{1,17},{17... | collective-permute-start | bytes 1572872 | tf_op jit(solution)/shard_map/ppermute | solution.py:652
  9.1 10.6 %collective-permute-start.1 = (bf16[64,32,128]{2,1,0:T(8,128)(2,1)}, bf16[64,32,128]{2,1,0:T(8,128)(2,1)S(1)}, u32[]{:S(2)}, u32[]{:S(2)}) collective-permute-start(bf16[64,32,128]{2,1,0:T(8,128)(2,1)} %get-tuple-element.20), channel_id=1, source_target_pairs={{16,0},{32,16},{48,32},{64,48},{80,64},{96,80},{112,96},{17,1},{33... | collective-permute-start | bytes 1572872 | tf_op jit(solution)/shard_map/ppermute | solution.py:653
  17.9 1.9 %copy-start = (bf16[64,32,128]{2,1,0:T(8,128)(2,1)}, bf16[64,32,128]{2,1,0:T(8,128)(2,1)S(1)}, u32[]{:S(2)}) copy-start(bf16[64,32,128]{2,1,0:T(8,128)(2,1)S(1)} %collective-permute-done.lo_hbm.from_lo.refs_7_) | copy-start | bytes 1572868
  19.7 0.8 copy-start.1
  22.2 33.7 %collective-permute-start.2 = (bf16[82,32,128]{2,1,0:T(8,128)(2,1)}, bf16[82,32,128]{2,1,0:T(8,128)(2,1)S(1)}, u32[]{:S(2)}, u32[]{:S(2)}) collective-permute-start(bf16[82,32,128]{2,1,0:T(8,128)(2,1)} %get-tuple-element.28), channel_id=1, source_target_pairs={{0,1},{1,2},{2,3},{3,4},{4,5},{5,6},{6,7},{7,8},{8,9},{9,10},{10,1... | collective-permute-start | bytes 2015240 | tf_op jit(solution)/shard_map/ppermute | solution.py:666
  25.7 30.2 %collective-permute-start.3 = (bf16[82,32,128]{2,1,0:T(8,128)(2,1)}, bf16[82,32,128]{2,1,0:T(8,128)(2,1)S(1)}, u32[]{:S(2)}, u32[]{:S(2)}) collective-permute-start(bf16[82,32,128]{2,1,0:T(8,128)(2,1)} %get-tuple-element.29), channel_id=1, source_target_pairs={{1,0},{2,1},{3,2},{4,3},{5,4},{6,5},{7,6},{8,7},{9,8},{10,9},{11,1... | collective-permute-start | bytes 2015240 | tf_op jit(solution)/shard_map/ppermute | solution.py:667
  28.1 27.8 %all-to-all-start = ((bf16[128,16,128]{2,1,0:T(8,128)(2,1)}), bf16[128,16,128]{2,1,0:T(8,128)(2,1)S(1)}, u32[]{:S(2)}, u32[]{:S(2)}) async-start(bf16[128,16,128]{2,1,0:T(8,128)(2,1)} %get-tuple-element.18), calls=%async_computation | async-start | bytes 1048576 | tf_op jit(solution)/shard_map/all_to_all | solution.py:654
  56.0 0.8 copy-start.2
  56.0 1.1 %copy-start.3 = (bf16[82,32,128]{2,1,0:T(8,128)(2,1)}, bf16[82,32,128]{2,1,0:T(8,128)(2,1)S(1)}, u32[]{:S(2)}) copy-start(bf16[82,32,128]{2,1,0:T(8,128)(2,1)S(1)} %collective-permute-done.2.refs_9_) | copy-start | bytes 2015236
  56.0 1.3 %copy-start.4 = (bf16[82,32,128]{2,1,0:T(8,128)(2,1)}, bf16[82,32,128]{2,1,0:T(8,128)(2,1)S(1)}, u32[]{:S(2)}) copy-start(bf16[82,32,128]{2,1,0:T(8,128)(2,1)S(1)} %collective-permute-done.3.refs_10_) | copy-start | bytes 2015236

commit v5 on v4

--- a/solution.py
+++ b/solution.py
@@ -10,7 +10,6 @@
 F32 = jnp.float32
 RANK = 64
 VEC = 32
-VMEM = pltpu.VMEM
 
 
 def dot_nt(a, b):
@@ -344,7 +343,7 @@
 
 
 def final_kernel(
-    counts_upper_ref, codes_upper_ref, *refs,
+    counts_hbm, codes_hbm, *refs,
 ):
     n_in = 14
     sources, coupling_hbm, out_ref = refs[:n_in], refs[n_in], refs[n_in + 1]
@@ -355,7 +354,7 @@
     ) = buffers
     (
     e0, e1, e2, e3, f4, f5, f6, shifted, b0, b1, b2, b3, cols, edge_col, out_buf, coupling_ref,
-    sems, in_sems, acc_sems, level_sems,
+    sems, in_sems, acc_sems, level_sems, counts_upper_ref, codes_upper_ref, list_sems,
     ) = rest
     patch = acc_ref.shape[0]
 
@@ -371,6 +370,12 @@
         )
 
     first = (9, 10, 12)
+    lists = [
+        pltpu.make_async_copy(counts_hbm, counts_upper_ref, list_sems.at[0]),
+        pltpu.make_async_copy(codes_hbm, codes_upper_ref, list_sems.at[1]),
+    ]
+    for copy_list in lists:
+        copy_list.start()
     fetch(1).start()
     fetch(0).start()
     fetch_level(4).start()
@@ -402,6 +407,8 @@
             return coupling_ref[level, d, :, bp * 128 : bp * 128 + 128]
         return shifted[level, d, :, bp * 128 : bp * 128 + 128]
 
+    for copy_list in lists:
+        copy_list.wait()
     fetch(0).wait()
     fetch(1).wait()
     get_level(4)
@@ -603,14 +610,6 @@
     lax.fori_loop(0, patch, loop_wait, 0)
 
 
-def vspec():
-    return pl.BlockSpec(memory_space=VMEM)
-
-
-def sspec():
-    return pl.BlockSpec(memory_space=pltpu.SMEM)
-
-
 def shards(
     samples, leaf_basis, transfer, coupling, near_tiles,
     codes_local, counts_local, codes_upper, counts_upper,
@@ -717,11 +716,14 @@
         pltpu.SemaphoreType.DMA((len(inputs) - 1,)),
         pltpu.SemaphoreType.DMA((patch,)),
         pltpu.SemaphoreType.DMA((5,)),
+        pltpu.SMEM(counts_upper.shape, jnp.int32),
+        pltpu.VMEM(codes_upper.shape[::-1], jnp.int32),
+        pltpu.SemaphoreType.DMA((2,)),
     ]
     return pl.pallas_call(
         final_kernel,
         out_shape=jax.ShapeDtypeStruct((patch, patch, VEC, 256), BF),
-        in_specs=[sspec(), vspec()] + [anywhere] * (len(inputs) + 1),
+        in_specs=[anywhere] * (len(inputs) + 3),
         out_specs=pl.BlockSpec(memory_space=pl.ANY),
         scratch_shapes=scratch,
         compiler_params=params,

time: 81.6 us -> 81.4 us (level)
  the two profiles are of different devices: /device:TPU:26 before, /device:TPU:27 now
where the time goes in v5:
time: 81.4 us; the launch traced here: 81.2 us
  Pallas kernels  47.9 us (59%)
  starting transfers between devices  20.6 us (25%)
  waiting for transfers between devices  10.5 us (13%)
  local copies, waits for them, and re-layouts  2.1 us (3%)
    pallas_call x1, Pallas kernels, shards(): pl.pallas_call(final_kernel, out_shape=jax.ShapeDtypeStruct((patch, patch...  23.9 us
    pallas_call x1, Pallas kernels, shards(): pl.pallas_call(near_kernel, out_shape=[jax.ShapeDtypeStruct((patch, patch...  15.1 us
    all_to_all x1, starting transfers between devices, shards(): every = lax.all_to_all(q4, ('gx', 'gy'), 0, 0, tiled=True)  9.7 us
    pallas_call x1, Pallas kernels, shards(): pl.pallas_call(project_kernel, out_shape=[jax.ShapeDtypeStruct(v, BF) for...  7.16 us
    ppermute x1, waiting for transfers between devices, shards(): from_lo = lax.ppermute(gx_hi, 'gx', up(n_gx))  4.49 us
    ppermute x1, waiting for transfers between devices, shards(): from_hi = lax.ppermute(gx_lo, 'gx', dn(n_gx))  4.29 us
    ppermute x1, starting transfers between devices, shards(): from_lo = lax.ppermute(gx_hi, 'gx', up(n_gx))  3.68 us
    ppermute x1, starting transfers between devices, shards(): from_left = lax.ppermute(send_right, 'gy', up(n_gy))  3.21 us
  transfers between devices with their start and end apart: 5, of which 3 were waited for; matrix products, arithmetic and copies ran while one was open for 0% of the time, Pallas kernels for 19%

profile of v5, /device:TPU:27, one launch (start us, length us, event | category | flops | bytes accessed | tf_op | source)
XLA Modules:
  0.0 81.2 jit_solution(12705914354157376306)
XLA Ops:
  0.0 7.2 %project.1 = (bf16[16,8,32,128]{3,2,1,0:T(8,128)(2,1)}, bf16[8,4,32,128]{3,2,1,0:T(8,128)(2,1)}, bf16[4,2,32,128]{3,2,1,0:T(8,128)(2,1)}, bf16[2,1,32,128]{3,2,1...) custom-call(bf16[16,16,32,256]{3,2,1,0:T(8,128)(2,1)} %s_hbm.1, ...), custom_call_target="tpu_custom_call" | custom-call | tf_op jit(solution)/shard_map/project/pallas_call | solution.py:629
  7.2 3.7 %collective-permute-start = (bf16[64,32,128]{2,1,0:T(8,128)(2,1)}, bf16[64,32,128]{2,1,0:T(8,128)(2,1)S(1)}, u32[]{:S(2)}, u32[]{:S(2)}) collective-permute-start(bf16[64,32,128]{2,1,0:T(8,128)(2,1)} %get-tuple-element.19), channel_id=1, source_target_pairs={{0,16},{16,32},{32,48},{48,64},{64,80},{80,96},{96,112},{1,17},{17... | collective-permute-start | bytes 1572872 | tf_op jit(solution)/shard_map/ppermute | solution.py:651
  10.9 1.9 %collective-permute-start.1 = (bf16[64,32,128]{2,1,0:T(8,128)(2,1)}, bf16[64,32,128]{2,1,0:T(8,128)(2,1)S(1)}, u32[]{:S(2)}, u32[]{:S(2)}) collective-permute-start(bf16[64,32,128]{2,1,0:T(8,128)(2,1)} %get-tuple-element.20), channel_id=1, source_target_pairs={{16,0},{32,16},{48,32},{64,48},{80,64},{96,80},{112,96},{17,1},{33... | collective-permute-start | bytes 1572872 | tf_op jit(solution)/shard_map/ppermute | solution.py:652
  12.8 4.5 %collective-permute-done.lo_hbm.from_lo.refs_7_ = bf16[64,32,128]{2,1,0:T(8,128)(2,1)S(1)} collective-permute-done((bf16[64,32,128]{2,1,0:T(8,128)(2,1)}, bf16[64,32,128]{2,1,0:T(8,128)(2,1)S(1)}, u32[]{:S(2)}, u32[]{:S(2)}) %collective-permute-start) | collective-permute-done | bytes 524320 | tf_op jit(solution)/shard_map/ppermute | solution.py:651
  17.3 0.0 copy-start
  17.3 4.3 %collective-permute-done.1.hi_hbm.from_hi.refs_8_ = bf16[64,32,128]{2,1,0:T(8,128)(2,1)S(1)} collective-permute-done((bf16[64,32,128]{2,1,0:T(8,128)(2,1)}, bf16[64,32,128]{2,1,0:T(8,128)(2,1)S(1)}, u32[]{:S(2)}, u32[]{:S(2)}) %collective-permute-start.1) | collective-permute-done | bytes 524320 | tf_op jit(solution)/shard_map/ppermute | solution.py:652
  21.6 0.0 copy-start.1
  21.6 0.0 copy-done
  21.6 0.8 copy-done.1
  22.4 1.7 %corner.1 = (bf16[82,32,128]{2,1,0:T(8,128)(2,1)}, bf16[82,32,128]{2,1,0:T(8,128)(2,1)}) custom-call(bf16[64,32,128]{2,1,0:T(8,128)(2,1)} %copy-done, bf16[64,32,128]{2,1,0:T(8,128)(2,1)} %copy-done.1, bf16[82,32,128]{2,1,0:T(8,128)(2,1)} %get-tuple-element.26.left_in, ...), custom_call_target="tpu_custom_call", output_to_operand_aliasing={{0}: (2, {}), {1}: (3, {})} | custom-call | tf_op jit(solution)/shard_map/corner/pallas_call | solution.py:655
  24.1 3.2 %collective-permute-start.2 = (bf16[82,32,128]{2,1,0:T(8,128)(2,1)}, bf16[82,32,128]{2,1,0:T(8,128)(2,1)S(1)}, u32[]{:S(2)}, u32[]{:S(2)}) collective-permute-start(bf16[82,32,128]{2,1,0:T(8,128)(2,1)} %get-tuple-element.28), channel_id=1, source_target_pairs={{0,1},{1,2},{2,3},{3,4},{4,5},{5,6},{6,7},{7,8},{8,9},{9,10},{10,1... | collective-permute-start | bytes 2015240 | tf_op jit(solution)/shard_map/ppermute | solution.py:665
  27.3 2.1 %collective-permute-start.3 = (bf16[82,32,128]{2,1,0:T(8,128)(2,1)}, bf16[82,32,128]{2,1,0:T(8,128)(2,1)S(1)}, u32[]{:S(2)}, u32[]{:S(2)}) collective-permute-start(bf16[82,32,128]{2,1,0:T(8,128)(2,1)} %get-tuple-element.29), channel_id=1, source_target_pairs={{1,0},{2,1},{3,2},{4,3},{5,4},{6,5},{7,6},{8,7},{9,8},{10,9},{11,1... | collective-permute-start | bytes 2015240 | tf_op jit(solution)/shard_map/ppermute | solution.py:666
  29.4 9.7 %all-to-all-start = ((bf16[128,16,128]{2,1,0:T(8,128)(2,1)}), bf16[128,16,128]{2,1,0:T(8,128)(2,1)S(1)}, u32[]{:S(2)}, u32[]{:S(2)}) async-start(bf16[128,16,128]{2,1,0:T(8,128)(2,1)} %get-tuple-element.18), calls=%async_computation | async-start | bytes 1048576 | tf_op jit(solution)/shard_map/all_to_all | solution.py:653
  39.1 15.1 %near.1 = (bf16[16,16,32,256]{3,2,1,0:T(8,128)(2,1)}, s32[2,344,128]{2,1,0:T(8,128)}) custom-call(bf16[16,16,32,256]{3,2,1,0:T(8,128)(2,1)} %s_hbm.1, bf16[9,256,256]{2,1,0:T(8,128)(2,1)} %refs_12_.1, s32[256,4,27]{2,1,0:T(4,128)} %bitcast.3, s32[16,4,16]{2,1,0:T(4,128)} %bitcast.4, bf16[64,32,128]{2,1,0:T(8,128)(2,1)} %copy-done, bf16[64,32,128]{2,1,0:T(8,128)(2,1)} %copy-done.1), custom_call_target="tpu_custom_call" | custom-call | tf_op jit(solution)/shard_map/near/pallas_call | solution.py:671
  54.2 1.7 %all-to-all-done.refs_1_ = bf16[128,16,128]{2,1,0:T(8,128)(2,1)S(1)} async-done(((bf16[128,16,128]{2,1,0:T(8,128)(2,1)}), bf16[128,16,128]{2,1,0:T(8,128)(2,1)S(1)}, u32[]{:S(2)}, u32[]{:S(2)}) %all-to-all-start) | async-done | bytes 524320 | tf_op jit(solution)/shard_map/all_to_all | solution.py:653
  56.0 0.0 copy-start.2
  56.0 0.0 collective-permute-done.2.refs_9_
  56.0 0.0 copy-start.3
  56.0 0.0 collective-permute-done.3.refs_10_
  56.0 0.0 copy-start.4
  56.0 0.8 copy-done.2
  56.8 0.3 copy-done.3
  57.0 0.2 copy-done.4
  57.3 23.9 %final.1 = bf16[16,16,32,256]{3,2,1,0:T(8,128)(2,1)} custom-call(s32[168]{0:T(256)} %counts_hbm.1, s32[27,168]{1,0:T(8,128)} %bitcast.5, bf16[5,64,256]{2,1,0:T(8,128)(2,1)} %refs_0_.1, bf16[128,16,128]{2,1,0:T(8,128)(2,1)} %copy-done.2, s32[2,344,128]{2,1,0:T(8,128)} %get-tuple-element.21.refs_2_, bf16[16,8,32,128]{3,2,1,0:T(8,128)(2,1)} %get-tuple-element.22.refs_3_, ...), custom_call_target="tpu_custom_call" | custom-call | tf_op jit(solution)/shard_map/final/pallas_call | solution.py:723
Async XLA Ops:
  7.2 10.1 %collective-permute-start = (bf16[64,32,128]{2,1,0:T(8,128)(2,1)}, bf16[64,32,128]{2,1,0:T(8,128)(2,1)S(1)}, u32[]{:S(2)}, u32[]{:S(2)}) collective-permute-start(bf16[64,32,128]{2,1,0:T(8,128)(2,1)} %get-tuple-element.19), channel_id=1, source_target_pairs={{0,16},{16,32},{32,48},{48,64},{64,80},{80,96},{96,112},{1,17},{17... | collective-permute-start | bytes 1572872 | tf_op jit(solution)/shard_map/ppermute | solution.py:651
  10.9 10.7 %collective-permute-start.1 = (bf16[64,32,128]{2,1,0:T(8,128)(2,1)}, bf16[64,32,128]{2,1,0:T(8,128)(2,1)S(1)}, u32[]{:S(2)}, u32[]{:S(2)}) collective-permute-start(bf16[64,32,128]{2,1,0:T(8,128)(2,1)} %get-tuple-element.20), channel_id=1, source_target_pairs={{16,0},{32,16},{48,32},{64,48},{80,64},{96,80},{112,96},{17,1},{33... | collective-permute-start | bytes 1572872 | tf_op jit(solution)/shard_map/ppermute | solution.py:652
  17.3 4.3 %copy-start = (bf16[64,32,128]{2,1,0:T(8,128)(2,1)}, bf16[64,32,128]{2,1,0:T(8,128)(2,1)S(1)}, u32[]{:S(2)}) copy-start(bf16[64,32,128]{2,1,0:T(8,128)(2,1)S(1)} %collective-permute-done.lo_hbm.from_lo.refs_7_) | copy-start | bytes 1572868
  21.6 0.8 copy-start.1
  24.1 31.9 %collective-permute-start.2 = (bf16[82,32,128]{2,1,0:T(8,128)(2,1)}, bf16[82,32,128]{2,1,0:T(8,128)(2,1)S(1)}, u32[]{:S(2)}, u32[]{:S(2)}) collective-permute-start(bf16[82,32,128]{2,1,0:T(8,128)(2,1)} %get-tuple-element.28), channel_id=1, source_target_pairs={{0,1},{1,2},{2,3},{3,4},{4,5},{5,6},{6,7},{7,8},{8,9},{9,10},{10,1... | collective-permute-start | bytes 2015240 | tf_op jit(solution)/shard_map/ppermute | solution.py:665
  27.3 28.7 %collective-permute-start.3 = (bf16[82,32,128]{2,1,0:T(8,128)(2,1)}, bf16[82,32,128]{2,1,0:T(8,128)(2,1)S(1)}, u32[]{:S(2)}, u32[]{:S(2)}) collective-permute-start(bf16[82,32,128]{2,1,0:T(8,128)(2,1)} %get-tuple-element.29), channel_id=1, source_target_pairs={{1,0},{2,1},{3,2},{4,3},{5,4},{6,5},{7,6},{8,7},{9,8},{10,9},{11,1... | collective-permute-start | bytes 2015240 | tf_op jit(solution)/shard_map/ppermute | solution.py:666
  29.4 26.6 %all-to-all-start = ((bf16[128,16,128]{2,1,0:T(8,128)(2,1)}), bf16[128,16,128]{2,1,0:T(8,128)(2,1)S(1)}, u32[]{:S(2)}, u32[]{:S(2)}) async-start(bf16[128,16,128]{2,1,0:T(8,128)(2,1)} %get-tuple-element.18), calls=%async_computation | async-start | bytes 1048576 | tf_op jit(solution)/shard_map/all_to_all | solution.py:653
  56.0 0.8 copy-start.2
  56.0 1.1 %copy-start.3 = (bf16[82,32,128]{2,1,0:T(8,128)(2,1)}, bf16[82,32,128]{2,1,0:T(8,128)(2,1)S(1)}, u32[]{:S(2)}) copy-start(bf16[82,32,128]{2,1,0:T(8,128)(2,1)S(1)} %collective-permute-done.2.refs_9_) | copy-start | bytes 2015236
  56.0 1.3 %copy-start.4 = (bf16[82,32,128]{2,1,0:T(8,128)(2,1)}, bf16[82,32,128]{2,1,0:T(8,128)(2,1)S(1)}, u32[]{:S(2)}) copy-start(bf16[82,32,128]{2,1,0:T(8,128)(2,1)S(1)} %collective-permute-done.3.refs_10_) | copy-start | bytes 2015236
